TPU v7x, 32 devices: a whole 2x2x4 slice. The times are simulated.
32 devices in a mesh: tp: 4 (over z), sp: 8 (over y, x, core).
Axes of the slice: x: 2, y: 2, z: 4, core: 2. Of those that a mesh axis runs over, the one named last changes fastest.
Arguments:
- x_tok: bfloat16 [256, 4096], replicated
- seq_lens: int32 [256], replicated
- k_cache: bfloat16 [256, 512, 8, 128], P(None, 'sp', 'tp')
- v_cache: bfloat16 [256, 512, 8, 128], P(None, 'sp', 'tp')
- g_attn: bfloat16 [4096], replicated
- w_q: bfloat16 [4096, 4096], P(None, 'tp')
- w_k: bfloat16 [4096, 1024], P(None, 'tp')
- w_v: bfloat16 [4096, 1024], P(None, 'tp')
- w_o: bfloat16 [4096, 4096], P('tp')
- g_mlp: bfloat16 [4096], replicated
- w_gate: bfloat16 [4096, 14336], P(None, 'tp')
- w_up: bfloat16 [4096, 14336], P(None, 'tp')
- w_down: bfloat16 [14336, 4096], P('tp')
Outputs:
- output 1: bfloat16 [256, 4096], replicated
- output 2: bfloat16 [256, 512, 8, 128], P(None, 'sp', 'tp')
- output 3: bfloat16 [256, 512, 8, 128], P(None, 'sp', 'tp')
All inputs are finite; a program needn't handle non-finite values.
Results may differ from a plain program's by a relative error of at most 0.0133669.
Values sent between devices are 32-bit elements.
A program may use at most 1 GiB of HBM per device.

v0:
```python
import jax
import jax.numpy as jnp
from jax import lax
from jax.sharding import PartitionSpec as P

ROPE_BASE = 500000.0
NORM_EPS = 1e-5


def rms_norm(x_in, norm_gain):
    x_f32 = x_in.astype(jnp.float32)
    inv_rms = lax.rsqrt(jnp.mean(x_f32 * x_f32, axis=-1, keepdims=True) + NORM_EPS)
    return (x_f32 * inv_rms * norm_gain.astype(jnp.float32)).astype(jnp.bfloat16)


def apply_rope(heads_in, positions):
    head_dim = heads_in.shape[-1]
    half_dim = head_dim // 2
    inv_freq = jnp.power(jnp.float32(ROPE_BASE), jnp.arange(half_dim, dtype=jnp.float32) * (-2.0 / head_dim))
    angles = positions.astype(jnp.float32)[:, None, None] * inv_freq
    cos_a = jnp.cos(angles)
    sin_a = jnp.sin(angles)
    heads_f32 = heads_in.astype(jnp.float32)
    first_half = heads_f32[..., :half_dim]
    second_half = heads_f32[..., half_dim:]
    rotated = jnp.concatenate([first_half * cos_a - second_half * sin_a, second_half * cos_a + first_half * sin_a], axis=-1)
    return rotated.astype(jnp.bfloat16)


def solution(mesh):
    cache_spec = P(None, "sp", "tp", None)
    col_spec = P(None, "tp")
    row_spec = P("tp", None)
    full_spec = P()

    def local_step(x_tok, seq_lens, k_blk, v_blk, g_attn, wq_loc, wk_loc, wv_loc, wo_loc, g_mlp, wg_loc, wu_loc, wd_loc):
        batch_rows, seq_blk, kv_loc, head_dim = k_blk.shape
        q_loc = wq_loc.shape[1] // head_dim
        groups = q_loc // kv_loc
        x_norm = rms_norm(x_tok, g_attn)
        q_new = jnp.dot(x_norm, wq_loc, preferred_element_type=jnp.float32).astype(jnp.bfloat16).reshape(batch_rows, q_loc, head_dim)
        k_new = jnp.dot(x_norm, wk_loc, preferred_element_type=jnp.float32).astype(jnp.bfloat16).reshape(batch_rows, kv_loc, head_dim)
        v_new = jnp.dot(x_norm, wv_loc, preferred_element_type=jnp.float32).astype(jnp.bfloat16).reshape(batch_rows, kv_loc, head_dim)
        q_rot = apply_rope(q_new, seq_lens)
        k_rot = apply_rope(k_new, seq_lens)
        local_pos = lax.axis_index("sp") * seq_blk + jnp.arange(seq_blk)
        is_new = (local_pos[None, :] == seq_lens[:, None])[:, :, None, None]
        k_out = jnp.where(is_new, k_rot[:, None], k_blk)
        v_out = jnp.where(is_new, v_new[:, None], v_blk)
        q_grp = q_rot.reshape(batch_rows, kv_loc, groups, head_dim)
        scores = jnp.einsum("bkgd,bskd->bkgs", q_grp, k_out, preferred_element_type=jnp.float32) * (head_dim ** -0.5)
        is_valid = (local_pos[None, :] <= seq_lens[:, None])[:, None, None, :]
        masked = jnp.where(is_valid, scores, -1e30)
        blk_max = jnp.max(masked, axis=-1, keepdims=True)
        weights = jnp.where(is_valid, jnp.exp(masked - blk_max), 0.0)
        blk_sum = jnp.sum(weights, axis=-1, keepdims=True)
        blk_mix = jnp.einsum("bkgs,bskd->bkgd", weights.astype(jnp.bfloat16), v_out, preferred_element_type=jnp.float32)
        glob_max = lax.pmax(blk_max, "sp")
        factor = jnp.exp(blk_max - glob_max)
        packed = lax.psum(jnp.concatenate([blk_mix * factor, blk_sum * factor], axis=-1), "sp")
        attn_out = (packed[..., :head_dim] / packed[..., head_dim:]).astype(jnp.bfloat16).reshape(batch_rows, q_loc * head_dim)
        attn_proj = lax.psum(jnp.dot(attn_out, wo_loc, preferred_element_type=jnp.float32), "tp")
        hidden = (x_tok.astype(jnp.float32) + attn_proj).astype(jnp.bfloat16)
        h_norm = rms_norm(hidden, g_mlp)
        gate_proj = jnp.dot(h_norm, wg_loc, preferred_element_type=jnp.float32).astype(jnp.bfloat16)
        up_proj = jnp.dot(h_norm, wu_loc, preferred_element_type=jnp.float32).astype(jnp.bfloat16)
        act_prod = (jax.nn.silu(gate_proj.astype(jnp.float32)) * up_proj.astype(jnp.float32)).astype(jnp.bfloat16)
        mlp_out = lax.psum(jnp.dot(act_prod, wd_loc, preferred_element_type=jnp.float32), "tp")
        y_out = (hidden.astype(jnp.float32) + mlp_out).astype(jnp.bfloat16)
        return y_out, k_out, v_out

    return jax.shard_map(local_step, mesh=mesh, in_specs=(full_spec, full_spec, cache_spec, cache_spec, full_spec, col_spec, col_spec, col_spec, row_spec, full_spec, col_spec, col_spec, row_spec), out_specs=(full_spec, cache_spec, cache_spec), check_vma=False)
```

profile of v0, /device:TPU:1, one launch (start us, length us, event | category | flops | bytes accessed | tf_op | source)
XLA Modules:
  0.0 522.2 jit_solution(17501848961830630895)
XLA Ops:
  7.2 0.0 copy-start
  7.2 0.0 all-reduce.4.cloned.1.call-start
  7.3 0.8 convert_element_type.85
  8.1 2.1 fusion.8
  10.2 0.7 convert_element_type.80
  10.9 0.8 broadcast_compare_fusion.1
  11.7 0.3 multiply_cosine_fusion
  12.0 0.1 copy.51
  12.1 0.1 copy.52
  12.2 2.7 convolution_convert_fusion.4
  14.9 0.0 copy-start.3
  15.0 0.1 copy.53
  15.2 3.5 convolution_convert_fusion.3
  18.6 0.1 copy.55
  18.8 5.7 %fusion.27 = f32[32,8,8,128]{3,1,2,0:T(8,128)S(1)} fusion(bf16[4096,1024]{1,0:T(8,128)(2,1)} %param.18, bf16[256,4096]{1,0:T(8,128)(2,1)S(1)} %copy-done.3, f32[4096]{0:T(1024)S(1)} %convert_element_type.80, f32[256]{0:T(256)S(1)} %add_rsqrt_fusion.1), kind=kOutput, calls=%fused_computation.35 | convolution fusion | flops 2152202240 | bytes 11551744 | tf_op jit(solution)/shard_map/dot_general | solution.py:41
  24.5 0.2 copy.63
  24.7 0.4 subtract_convert_fusion
  25.2 26.6 %broadcast_select_fusion = (bf16[256,64,2,128]{3,2,1,0:T(2,128)(2,1)}, bf16[256,64,2,128]{3,2,1,0:T(2,128)(2,1)S(1)}) fusion(bf16[256,64,2,128]{3,2,1,0:T(2,128)(2,1)} %param.16, pred[256,64]{1,0:T(8,128)(4,1)S(1)} %get-tuple-element.14, bf16[256,2,128]{2,1,0:T(2,128)(2,1)S(1)} %copy.55, bf16[256,64,2,128]{3,2,1,0:T(2,128)(2,1)} %param.15, ...), kind=kLoop, calls=%fused_computation | loop fusion | flops 8388608 | bytes 33832960 | tf_op jit(solution)/shard_map/jit(_where)/select_n | solution.py:49
  51.8 0.0 copy-start.2
  51.8 5.2 fusion.52
  57.0 0.1 copy.57
  57.1 13.0 %pmax.7 = f32[256,2,4,1]{0,2,3,1:T(4,128)S(1)} all-reduce(f32[256,2,4,1]{0,2,3,1:T(4,128)S(1)} %bitcast.29), channel_id=1, replica_groups=mesh['tp'=4,'sp'=8] {'sp'}, use_global_device_ids=true, to_apply=%region_2.3 | all-reduce | flops 2048 | bytes 16384 | tf_op jit(solution)/shard_map/pmax | solution.py:58
  70.1 1.4 fusion.32
  71.5 0.1 copy.59
  71.7 0.2 copy.58
  71.9 0.5 copy.60
  72.4 6.2 %fusion.23 = f32[256,2,4,128]{3,2,1,0:T(4,128)S(1)} fusion(bf16[256,64,2,128]{3,2,1,0:T(2,128)(2,1)} %get-tuple-element.9, f32[256,2,4,64]{3,2,1,0:T(4,128)S(1)} %get-tuple-element.18, f32[256,2,4]{2,1,0:T(2,128)S(1)} %copy.58, f32[256,2,4]{2,1,0:T(2,128)S(1)} %get-tuple-element.17, pred[256,64]{1,0:T(8,128)(4,1)S(1)} %get-tuple-element.13), kind=kOutput, calls=%fused_computation.32 | convolution fusion | flops 34209792 | bytes 9994240 | tf_op jit(solution)/shard_map/bkgs,bskd->bkgd/dot_general | solution.py:57
  78.6 1.8 pad_maximum_fusion
  80.4 0.0 all-reduce.4.cloned.1.call-update
  80.4 0.0 all-reduce.6.cloned.1.call-start
  80.5 61.6 %all-reduce.4.cloned.1.call-done = f32[256,2,4,129]{3,2,1,0:T(4,128)} async-done(((f32[256,2,4,129]{3,2,1,0:T(4,128)}), f32[256,2,4,129]{3,2,1,0:T(4,128)}) %all-reduce.4.cloned.1.call-update) | async-done | bytes 1056784 | tf_op jit(solution)/shard_map/psum | solution.py:60
  142.1 1.4 slice.29
  143.5 0.5 copy.61
  144.0 0.2 copy.62
  144.2 1.8 fusion.31
  146.0 0.4 reshape.167
  146.3 7.7 %fusion.53 = f32[256,4096]{1,0:T(8,128)} fusion(bf16[256,1024]{1,0:T(8,128)(2,1)S(1)} %reshape.167, bf16[1024,4096]{1,0:T(8,128)(2,1)} %param.21), kind=kOutput, calls=%fused_computation.70 | convolution fusion | flops 2147483648 | bytes 13107200 | tf_op jit(solution)/shard_map/dot_general | solution.py:62
  154.0 0.0 all-reduce.6.cloned.1.call-update
  154.1 0.3 all-reduce.8.cloned.1.call-start
  154.3 0.4 copy-done.6
  154.7 153.2 %all-reduce.6.cloned.1.call-done = f32[256,4096]{1,0:T(8,128)} async-done(((f32[256,4096]{1,0:T(8,128)}), f32[256,4096]{1,0:T(8,128)}) %all-reduce.6.cloned.1.call-update) | async-done | bytes 4194320 | tf_op jit(solution)/shard_map/psum | solution.py:62
  308.0 3.0 fusion.12
  311.0 1.3 copy-done.5
  312.3 15.2 %fusion.7 = f32[256,3584]{1,0:T(8,128)} fusion(bf16[4096,3584]{1,0:T(8,128)(2,1)} %param.23, bf16[256,4096]{1,0:T(8,128)(2,1)S(1)} %get-tuple-element.4, f32[4096]{0:T(1024)S(1)} %convert_element_type.94, f32[256]{0:T(256)S(1)} %add_rsqrt_fusion), kind=kOutput, calls=%fused_computation.17 | convolution fusion | flops 7522222080 | bytes 35144704 | tf_op jit(solution)/shard_map/dot_general | solution.py:65
  327.5 30.3 %fusion.16 = f32[256,4096]{1,0:T(8,128)} fusion(bf16[3584,4096]{1,0:T(8,128)(2,1)} %param.25, bf16[4096,3584]{1,0:T(8,128)(2,1)} %param.24, f32[256,3584]{1,0:T(8,128)} %fusion.7, bf16[256,4096]{1,0:T(8,128)(2,1)} %copy-done.5, f32[4096]{0:T(1024)S(1)} %convert_element_type.94, f32[256]{0:T(256)S(1)} %add_rsqrt_fusion), kind=kOutput, calls=%fused_computation.26 | convolution fusion | flops 15043919872 | bytes 68699136 | tf_op jit(solution)/shard_map/dot_general | solution.py:68
  357.9 0.0 all-reduce.8.cloned.1.call-update
  357.9 153.0 %all-reduce.8.cloned.1.call-done = f32[256,4096]{1,0:T(8,128)} async-done(((f32[256,4096]{1,0:T(8,128)}), f32[256,4096]{1,0:T(8,128)}) %all-reduce.8.cloned.1.call-update) | async-done | bytes 4194320 | tf_op jit(solution)/shard_map/psum | solution.py:68
  510.9 4.7 fusion.15
  (18 shorter events, 0.1 us)
Async XLA Ops:
  7.2 5.0 copy-start
  7.2 135.0 %all-reduce.4.cloned.1.call-start = ((), (), s32[]{:S(2)}) async-start(), calls=%async_computation | async-start | bytes 4194304 | tf_op jit(solution)/shard_map/psum | solution.py:60
  14.9 3.8 copy-start.3
  51.8 5.2 copy-start.2
  80.4 227.5 %all-reduce.6.cloned.1.call-start = ((), (), s32[]{:S(2)}) async-start(), calls=%async_computation.1 | async-start | bytes 8388608 | tf_op jit(solution)/shard_map/psum | solution.py:62
  154.0 0.7 copy-start.6
  154.0 153.9 %copy-start.4 = (bf16[256,4096]{1,0:T(8,128)(2,1)S(1)}, bf16[256,4096]{1,0:T(8,128)(2,1)}, u32[]{:S(2)}) copy-start(bf16[256,4096]{1,0:T(8,128)(2,1)} %param.13) | copy-start | bytes 6291460
  154.1 356.9 %all-reduce.8.cloned.1.call-start = ((), (), s32[]{:S(2)}) async-start(), calls=%async_computation.2 | async-start | bytes 8388608 | tf_op jit(solution)/shard_map/psum | solution.py:68
  311.0 1.3 copy-start.5
  357.9 157.8 %copy-start.1 = (bf16[4096,256]{1,0:T(8,128)(2,1)S(1)}, bf16[4096,256]{1,0:T(8,128)(2,1)}, u32[]{:S(2)}) copy-start(bf16[4096,256]{1,0:T(8,128)(2,1)} %param.19) | copy-start | bytes 6291460
Sparse Core Ops, SparseCore 0:
  80.6 61.5 all-reduce.3
  154.2 153.7 all-reduce.5
  358.0 152.8 all-reduce.7
where the time goes:
time: 524 us; the launch traced here: 522 us
  waiting for transfers between devices  368 us (70%)
  matrix products  76.6 us (15%)
  other arithmetic  44.7 us (9%)
  between operations  14 us (3%)
  blocking collectives  13 us (2%)
  local copies, waits for them, and re-layouts  5.71 us (1%)
    psum x1, waiting for transfers between devices, local_step(): lax.psum(jnp.dot(attn_out, wo_loc, preferred_element_type=jnp.float32), '...  153 us
    psum x1, waiting for transfers between devices, local_step(): lax.psum(jnp.dot(act_prod, wd_loc, preferred_element_type=jnp.float32), '...  153 us
    psum x1, waiting for transfers between devices, local_step(): lax.psum(jnp.concatenate([blk_mix * factor, blk_sum * factor], axis=-1),...  61.6 us
    dot_general x1, matrix products, local_step(): jnp.dot(act_prod, wd_loc, preferred_element_type=jnp.float32)  30.3 us
    select_n x1, other arithmetic, local_step(): v_out = jnp.where(is_new, v_new[:, None], v_blk)  26.6 us
    dot_general x1, matrix products, local_step(): jnp.dot(h_norm, wg_loc, preferred_element_type=jnp.float32)  15.2 us
    pmax x1, blocking collectives, local_step(): glob_max = lax.pmax(blk_max, 'sp')  13 us
  transfers between devices with their start and end apart: 3, of which 3 were waited for; matrix products, arithmetic and copies ran while one was open for 0% of the time, Pallas kernels for 0%

commit v1 on v0

v1 whole, which is shorter than its diff:
```python
import functools

import jax
import jax.numpy as jnp
from jax import lax
from jax.experimental import pallas as pl
from jax.experimental.pallas import tpu as pltpu
from jax.sharding import PartitionSpec as P

ROPE_BASE = 500000.0
NORM_EPS = 1e-5
MESH = pl.DeviceIdType.MESH
F32 = jnp.float32
BF16 = jnp.bfloat16
ANY = pl.BlockSpec(memory_space=pl.ANY)
VMEM = pl.BlockSpec(memory_space=pltpu.VMEM)
NEG = -1e30
BLK = 256


def qkv_kernel(x_hbm, g_ref, cos_ref, sin_ref, wq_hbm, wk_hbm, wv_hbm, q_ref, k_ref, v_ref, x_buf, u_buf, w_buf, x_sem, w_sem):
    rows = x_buf.shape[0]
    dim = x_buf.shape[1]
    nq = wq_hbm.shape[1] // BLK
    heads = wq_hbm.shape[1] // 128
    copies = [pltpu.make_async_copy(wq_hbm.at[:, pl.ds(i * BLK, BLK)], w_buf.at[i], w_sem.at[i]) for i in range(nq)]
    copies.append(pltpu.make_async_copy(wk_hbm, w_buf.at[nq], w_sem.at[nq]))
    copies.append(pltpu.make_async_copy(wv_hbm, w_buf.at[nq + 1], w_sem.at[nq + 1]))
    x_copy = pltpu.make_async_copy(x_hbm, x_buf, x_sem)
    x_copy.start()
    for cp in copies:
        cp.start()
    x_copy.wait()
    gain = g_ref[...]

    def norm(i, carry):
        at = pl.ds(pl.multiple_of(i * 16, 16), 16)
        xf = x_buf[at, :].astype(F32)
        inv = lax.rsqrt(jnp.sum(xf * xf, axis=-1, keepdims=True) * (1.0 / dim) + NORM_EPS)
        u_buf[at, :] = (xf * inv * gain).astype(BF16)
        return carry

    lax.fori_loop(0, rows // 16, norm, 0)
    cosv = cos_ref[...]
    sinv = sin_ref[...]

    def rope(h):
        h = h.astype(BF16).astype(F32)
        return (h * cosv + pltpu.roll(h, 64, 1) * sinv).astype(BF16).astype(F32)

    for i in range(nq + 2):
        copies[i].wait()
        prod = jnp.dot(u_buf[...], w_buf[i], preferred_element_type=F32)
        for s in range(2):
            part = prod[:, s * 128 : (s + 1) * 128]
            if i < nq:
                q_ref[pl.ds(2 * i + s, rows, stride=heads), :] = rope(part)
            elif i == nq:
                k_ref[pl.ds(s, rows, stride=2), :] = rope(part)
            else:
                v_ref[pl.ds(s, rows, stride=2), :] = part.astype(BF16).astype(F32)


def qkv(x, g, cosv, sinv, wq, wk, wv):
    rows, dim = x.shape
    heads = wq.shape[1] // 128
    nblk = wq.shape[1] // BLK + 2
    return pl.pallas_call(
        qkv_kernel,
        out_shape=(
            jax.ShapeDtypeStruct((rows * heads, 128), F32),
            jax.ShapeDtypeStruct((rows * 2, 128), F32),
            jax.ShapeDtypeStruct((rows * 2, 128), F32),
        ),
        in_specs=[ANY, VMEM, VMEM, VMEM, ANY, ANY, ANY],
        out_specs=(VMEM, VMEM, VMEM),
        scratch_shapes=[
            pltpu.VMEM((rows, dim), BF16),
            pltpu.VMEM((rows, dim), BF16),
            pltpu.VMEM((nblk, dim, BLK), BF16),
            pltpu.SemaphoreType.DMA,
            pltpu.SemaphoreType.DMA((nblk,)),
        ],
        compiler_params=pltpu.CompilerParams(vmem_limit_bytes=63_000_000),
        cost_estimate=pl.CostEstimate(flops=2 * rows * dim * nblk * BLK, bytes_accessed=2 * dim * nblk * BLK, transcendentals=0),
        name="qkv",
    )(x, g, cosv, sinv, wq, wk, wv)


def attn_kernel(lens_ref, q_ref, kn_ref, vn_ref, k_ref, v_ref, ko_ref, vo_ref, out_ref):
    nreq = k_ref.shape[0]
    base = lax.axis_index("sp") * 64
    g = pl.program_id(0)
    lane = lax.broadcasted_iota(jnp.int32, (8, 128), 1)
    head = lax.broadcasted_iota(jnp.int32, (8, 128), 0)
    match = (lane % 2) == (head // 4)
    lane_pos = jnp.where(match, lane // 2, 1 << 20)
    row_pos = (lax.broadcasted_iota(jnp.int32, (8, 16, 128), 0) * 8 + lax.broadcasted_iota(jnp.int32, (8, 16, 128), 1) // 2).astype(F32).astype(BF16)
    odd = (lax.broadcasted_iota(jnp.int32, (16, 128), 0) % 2) == 1
    scale = 128.0**-0.5
    zero = jnp.zeros((8, 128), BF16)

    def update(c_ref, n_ref, o_ref, b, pos_b):
        row0 = jnp.broadcast_to(n_ref[pl.ds(2 * b, 1), :], (16, 128))
        row1 = jnp.broadcast_to(n_ref[pl.ds(2 * b + 1, 1), :], (16, 128))
        new = jnp.where(odd, row1, row0).astype(BF16)
        upd = jnp.where(row_pos == pos_b, new[None], c_ref[b])
        o_ref[b] = upd
        return upd.reshape(128, 128)

    def step(it, carry):
        stm, stl = carry
        for pair in range(4):
            keys, vals, poss = [], [], []
            first = it * 8 + pair * 2
            for j in range(2):
                b = first + j
                pos = lens_ref[g * nreq + b] - base
                pos_b = jnp.full((8, 16, 128), pos, jnp.int32).astype(F32).astype(BF16)
                keys.append(update(k_ref, kn_ref, ko_ref, b, pos_b))
                vals.append(update(v_ref, vn_ref, vo_ref, b, pos_b))
                poss.append(pos)
            qrow = pl.multiple_of(first * 8, 16)
            qp = q_ref[pl.ds(qrow, 16), :].astype(BF16)
            sc = lax.dot_general(qp, jnp.concatenate(keys, axis=0), (((1,), (1,)), ((), ())), preferred_element_type=F32) * scale
            wts = []
            for j in range(2):
                s = sc[8 * j : 8 * j + 8, 128 * j : 128 * j + 128]
                valid = lane_pos <= poss[j]
                m = jnp.max(jnp.where(valid, s, NEG), axis=1, keepdims=True)
                w = jnp.where(valid, jnp.exp(s - m), 0.0)
                here = lane == first + j
                stm = jnp.where(here, m, stm)
                stl = jnp.where(here, jnp.sum(w, axis=1, keepdims=True), stl)
                wts.append(w.astype(BF16))
            wp = jnp.concatenate([jnp.concatenate([wts[0], zero], axis=1), jnp.concatenate([zero, wts[1]], axis=1)], axis=0)
            out_ref[0, pl.ds(qrow, 16), :] = jnp.dot(wp, jnp.concatenate(vals, axis=0), preferred_element_type=F32)
        return stm, stl

    stm, stl = lax.fori_loop(0, nreq // 8, step, (jnp.zeros((8, 128), F32), jnp.ones((8, 128), F32)))
    out_ref[0, pl.ds(nreq * 8, 8), :] = stm
    out_ref[0, pl.ds(nreq * 8 + 8, 8), :] = stl


def attn(lens, q, kn, vn, k, v):
    batch = k.shape[0]
    nreq = 32
    steps = batch // nreq
    cache = pl.BlockSpec((nreq, 8, 16, 128), lambda i, *_: (i, 0, 0, 0))
    return pl.pallas_call(
        attn_kernel,
        grid_spec=pltpu.PrefetchScalarGridSpec(
            num_scalar_prefetch=1,
            grid=(steps,),
            in_specs=[
                pl.BlockSpec((nreq * 8, 128), lambda i, *_: (i, 0)),
                pl.BlockSpec((nreq * 2, 128), lambda i, *_: (i, 0)),
                pl.BlockSpec((nreq * 2, 128), lambda i, *_: (i, 0)),
                cache,
                cache,
            ],
            out_specs=[cache, cache, pl.BlockSpec((1, nreq * 8 + 16, 128), lambda i, *_: (i, 0, 0))],
        ),
        out_shape=[
            jax.ShapeDtypeStruct(k.shape, BF16),
            jax.ShapeDtypeStruct(v.shape, BF16),
            jax.ShapeDtypeStruct((steps, nreq * 8 + 16, 128), F32),
        ],
        compiler_params=pltpu.CompilerParams(vmem_limit_bytes=63_000_000, dimension_semantics=("arbitrary",)),
        cost_estimate=pl.CostEstimate(flops=batch * 2**20, bytes_accessed=8 * k.size, transcendentals=0),
        name="attn",
    )(lens, q, kn, vn, k, v)


def merge(blocks, out_ref, rows, last):
    maxs = [b[rows : rows + 8, :] for b in blocks]
    top = functools.reduce(jnp.maximum, maxs)
    facs = [jnp.exp(m - top) for m in maxs]
    tot = functools.reduce(jnp.add, [f * b[rows + 8 : rows + 16, :] for f, b in zip(facs, blocks)])
    if last:
        inv = 1.0 / tot
        facs = [f * inv for f in facs]
    else:
        out_ref[rows : rows + 8, :] = top
        out_ref[rows + 8 : rows + 16, :] = tot
    for i in range(rows // 8):
        at = slice(8 * i, 8 * i + 8)
        out_ref[at, :] = functools.reduce(jnp.add, [b[at, :] * f[:, i : i + 1] for f, b in zip(facs, blocks)])


def tail_kernel(
    att_ref, x_hbm, g_ref, wo_hbm, wg_hbm, wu_hbm, wd_hbm, y_ref,
    d1_buf, m_buf, r1_buf, o_buf, p_buf, z1_buf, h_buf, hb_buf, a_buf, p2_buf, d2_buf, s2_buf, z2_buf, yg_buf, x_buf, hid_buf,
    wo_buf, wg_buf, wu_buf, wd_buf,
    lsem, gsem, usem, dsem, d1s, d1r, r1s, r1r, z1s, z1r, hs, hr, hds, hdr, d2s, d2r, z2s, z2r, ys, yr, ydr,
):
    tp, sp = lax.axis_index("tp"), lax.axis_index("sp")
    core, chip = sp % 2, sp // 2
    cx, cy = chip % 2, chip // 2
    mate = {"tp": tp, "sp": 2 * chip + (1 - core)}
    plane = [(chip + k) % 4 for k in range(4)]
    plane_id = [{"tp": tp, "sp": 2 * q + core} for q in plane]
    zs = [(tp + k) % 4 for k in range(4)]
    z_id = [{"tp": z, "sp": sp} for z in zs]
    rows = att_ref.shape[1] - 16
    dim = x_buf.shape[1]
    ring = wg_buf.shape[0]
    half = wd_buf.shape[1]
    nff = half // BLK
    ndn = wd_buf.shape[0]
    dcol = wd_buf.shape[2]

    me8 = pl.multiple_of(32 * sp + 8 * tp, 8)
    x_copy = pltpu.make_async_copy(x_hbm.at[pl.ds(me8, 8), :], x_buf, lsem.at[0])
    wo_copy = pltpu.make_async_copy(wo_hbm, wo_buf, lsem.at[1])

    def ff_copies(j, slot):
        at = pl.ds(pl.multiple_of(core * half + j * BLK, BLK), BLK)
        return (
            pltpu.make_async_copy(wg_hbm.at[:, at], wg_buf.at[slot], gsem.at[slot]),
            pltpu.make_async_copy(wu_hbm.at[:, at], wu_buf.at[slot], usem.at[slot]),
        )

    def dn_copy(j):
        return pltpu.make_async_copy(
            wd_hbm.at[pl.ds(pl.multiple_of(core * half, BLK), half), pl.ds(pl.multiple_of(j * dcol, dcol), dcol)], wd_buf.at[j], dsem.at[j]
        )

    wo_copy.start()
    x_copy.start()
    for j in range(min(ring, nff)):
        for cp in ff_copies(j, j):
            cp.start()
    for j in range(ndn):
        dn_copy(j).start()

    bar = pltpu.get_barrier_semaphore()
    for dev in [mate] + plane_id[1:] + z_id[1:]:
        pl.semaphore_signal(bar, inc=1, device_id=dev, device_id_type=MESH)
    pl.semaphore_wait(bar, 7)

    def send(src, dst, ssem, rsem, dev):
        cp = pltpu.make_async_remote_copy(src_ref=src, dst_ref=dst, send_sem=ssem, recv_sem=rsem, device_id=dev, device_id_type=MESH)
        cp.start()
        return cp

    order = [1, 2, 3, 0]
    d1 = {k: send(att_ref.at[2 * plane[k] + (1 - core)], d1_buf.at[k], d1s.at[k], d1r.at[k], mate) for k in order}
    r1 = {}
    for k in order:
        d1[k].wait_recv()
        merge([att_ref.at[2 * plane[k] + core], d1_buf.at[k]], m_buf.at[k], rows, False)
        if k:
            r1[k] = send(m_buf.at[k], r1_buf.at[k - 1], r1s.at[k - 1], r1r.at[k - 1], plane_id[k])
    for k in (1, 2, 3):
        r1[k].wait_recv()
    merge([m_buf.at[0]] + [r1_buf.at[k] for k in range(3)], o_buf, rows, True)

    nreq = rows // 8
    o = jnp.concatenate([o_buf[pl.ds(h, nreq, stride=8), :].astype(BF16) for h in range(8)], axis=1)
    wo_copy.wait()

    def proj(j, carry):
        at = pl.ds(pl.multiple_of(j * 512, 512), 512)
        p_buf[:, at] = jnp.dot(o, wo_buf[:, at], preferred_element_type=F32)
        return carry

    lax.fori_loop(0, dim // 512, proj, 0)

    def z_scatter(src, buf, ss, rs):
        return [send(src.at[pl.ds(pl.multiple_of(8 * zs[k], 8), 8), :], buf.at[k - 1], ss.at[k - 1], rs.at[k - 1], z_id[k]) for k in (1, 2, 3)]

    own = pl.ds(pl.multiple_of(8 * tp, 8), 8)
    z1 = z_scatter(p_buf, z1_buf, z1s, z1r)
    x_copy.wait()
    for cp in z1:
        cp.wait_recv()
    hid = (x_buf[...].astype(F32) + (p_buf[own, :] + z1_buf[0] + z1_buf[1] + z1_buf[2])).astype(BF16).astype(F32)
    hid_buf[...] = hid
    inv = lax.rsqrt(jnp.sum(hid * hid, axis=-1, keepdims=True) * (1.0 / dim) + NORM_EPS)
    mine = core * 4
    h_buf[mine + tp] = (hid * inv * g_ref[...]).astype(BF16).astype(F32)

    hz = [send(h_buf.at[mine + tp], h_buf.at[mine + tp], hs.at[k - 1], hr.at[k - 1], z_id[k]) for k in (1, 2, 3)]
    hd = [send(h_buf.at[mine + tp], h_buf.at[mine + tp], hds.at[0], hdr.at[0], mate)]
    for k in (1, 2, 3):
        hz[k - 1].wait_recv()
        slot = mine + (tp + 4 - k) % 4
        hd.append(send(h_buf.at[slot], h_buf.at[slot], hds.at[k], hdr.at[k], mate))
    for cp in hd:
        cp.wait_recv()
    for i in range(4):
        hb_buf[16 * i : 16 * i + 16, :] = jnp.concatenate([h_buf[2 * i], h_buf[2 * i + 1]], axis=0).astype(BF16)

    def ff(j, carry):
        slot = lax.rem(j, ring)
        for cp in ff_copies(j, slot):
            cp.wait()
        gate = jnp.dot(hb_buf[...], wg_buf[slot], preferred_element_type=F32).astype(BF16).astype(F32)
        up = jnp.dot(hb_buf[...], wu_buf[slot], preferred_element_type=F32).astype(BF16).astype(F32)
        a_buf[:, pl.ds(pl.multiple_of(j * BLK, BLK), BLK)] = (gate * jax.nn.sigmoid(gate) * up).astype(BF16)

        @pl.when(j + ring < nff)
        def _():
            for cp in ff_copies(j + ring, slot):
                cp.start()

        return carry

    lax.fori_loop(0, nff, ff, 0)

    def down(j, carry):
        dn_copy(j).wait()
        p2_buf[:, pl.ds(pl.multiple_of(j * dcol, dcol), dcol)] = jnp.dot(a_buf[...], wd_buf[j], preferred_element_type=F32)
        return carry

    lax.fori_loop(0, ndn, down, 0)

    d2 = send(p2_buf.at[pl.ds(pl.multiple_of(32 * (1 - core), 32), 32), :], d2_buf, d2s, d2r, mate)
    d2.wait_recv()
    s2_buf[...] = p2_buf[pl.ds(pl.multiple_of(32 * core, 32), 32), :] + d2_buf[...]
    z2 = z_scatter(s2_buf, z2_buf, z2s, z2r)
    for cp in z2:
        cp.wait_recv()

    xn = 2 * cy + (1 - cx)
    yn = 2 * (1 - cy) + cx
    dg = 2 * (1 - cy) + (1 - cx)
    xn_id, yn_id = {"tp": tp, "sp": 2 * xn + core}, {"tp": tp, "sp": 2 * yn + core}

    def block(c, k):
        return yg_buf.at[4 * (2 * c + core) + (tp + k) % 4]

    started = []

    def pass_on(c, k, dev, rs):
        started.append(send(block(c, k), block(c, k), ys.at[len(started)], rs, dev))

    def landed(c, k, rs):
        pltpu.make_async_copy(block(c, k), block(c, k), rs).wait()

    yg_buf[4 * sp + tp] = (hid_buf[...] + (s2_buf[own, :] + z2_buf[0] + z2_buf[1] + z2_buf[2])).astype(BF16).astype(F32)
    for k in (1, 2, 3):
        pass_on(chip, 0, z_id[k], yr.at[(4 - k) % 4])
    pass_on(chip, 0, xn_id, yr.at[4])
    pass_on(chip, 0, yn_id, yr.at[8])
    pass_on(chip, 0, mate, ydr.at[0])

    def around(k):
        landed(xn, k, yr.at[4 + k])
        if k % 2 == 0:
            pass_on(xn, k, yn_id, yr.at[12 + k])
        pass_on(xn, k, mate, ydr.at[4 + k])
        landed(yn, k, yr.at[8 + k])
        if k % 2 == 1:
            pass_on(yn, k, xn_id, yr.at[12 + k])
        pass_on(yn, k, mate, ydr.at[8 + k])

    for k in (1, 2, 3):
        landed(chip, k, yr.at[k])
        pass_on(chip, k, xn_id, yr.at[4 + k])
        pass_on(chip, k, yn_id, yr.at[8 + k])
        pass_on(chip, k, mate, ydr.at[k])
        around(k - 1)
    around(3)
    for k in range(4):
        landed(dg, k, yr.at[12 + k])
        pass_on(dg, k, mate, ydr.at[12 + k])
    for i, c in enumerate((chip, xn, yn, dg)):
        for k in range(4):
            other = yg_buf.at[4 * (2 * c + (1 - core)) + (tp + k) % 4]
            pltpu.make_async_copy(other, other, ydr.at[4 * i + k]).wait()

    def out(i, carry):
        y_ref[pl.ds(pl.multiple_of(i * 16, 16), 16), :] = jnp.concatenate([yg_buf[2 * i], yg_buf[2 * i + 1]], axis=0).astype(BF16)
        return carry

    lax.fori_loop(0, yg_buf.shape[0] // 2, out, 0)
    for cp in list(d1.values()) + list(r1.values()) + z1 + hz + hd + [d2] + z2 + started:
        cp.wait_send()


def tail(att, x, g, wo, wg, wu, wd):
    batch, dim = x.shape
    groups, rows16, _ = att.shape
    half = wg.shape[1] // 2
    ring = min(4, half // BLK)
    ndn = 8
    dma = pltpu.SemaphoreType.DMA
    return pl.pallas_call(
        tail_kernel,
        out_shape=jax.ShapeDtypeStruct((batch, dim), BF16),
        in_specs=[VMEM, ANY, VMEM, ANY, ANY, ANY, ANY],
        out_specs=VMEM,
        scratch_shapes=[
            pltpu.VMEM((4, rows16, 128), F32),
            pltpu.VMEM((4, rows16, 128), F32),
            pltpu.VMEM((3, rows16, 128), F32),
            pltpu.VMEM((rows16 - 16, 128), F32),
            pltpu.VMEM((32, dim), F32),
            pltpu.VMEM((3, 8, dim), F32),
            pltpu.VMEM((8, 8, dim), F32),
            pltpu.VMEM((64, dim), BF16),
            pltpu.VMEM((64, half), BF16),
            pltpu.VMEM((64, dim), F32),
            pltpu.VMEM((32, dim), F32),
            pltpu.VMEM((32, dim), F32),
            pltpu.VMEM((3, 8, dim), F32),
            pltpu.VMEM((batch // 8, 8, dim), F32),
            pltpu.VMEM((8, dim), BF16),
            pltpu.VMEM((8, dim), F32),
            pltpu.VMEM(wo.shape, BF16),
            pltpu.VMEM((ring, dim, BLK), BF16),
            pltpu.VMEM((ring, dim, BLK), BF16),
            pltpu.VMEM((ndn, half, dim // ndn), BF16),
            dma((2,)), dma((ring,)), dma((ring,)), dma((ndn,)),
            dma((4,)), dma((4,)), dma((3,)), dma((3,)), dma((3,)), dma((3,)),
            dma((3,)), dma((3,)), dma((4,)), dma((4,)), dma, dma, dma((3,)), dma((3,)),
            dma((40,)), dma((16,)), dma((16,)),
        ],
        compiler_params=pltpu.CompilerParams(collective_id=0, has_side_effects=True, vmem_limit_bytes=63_000_000),
        cost_estimate=pl.CostEstimate(flops=2 * 64 * dim * half * 3, bytes_accessed=6 * dim * half, transcendentals=0),
        name="tail",
    )(att, x, g, wo, wg, wu, wd)


def solution(mesh):
    cache_spec = P(None, "sp", "tp", None)
    col_spec = P(None, "tp")
    row_spec = P("tp", None)
    full_spec = P()

    def local_step(x_tok, seq_lens, k_blk, v_blk, g_attn, wq, wk, wv, wo, g_mlp, wg, wu, wd):
        batch = x_tok.shape[0]
        inv_freq = jnp.power(jnp.float32(ROPE_BASE), jnp.arange(64, dtype=F32) * (-2.0 / 128))
        angles = seq_lens.astype(F32)[:, None] * inv_freq
        cos_a, sin_a = jnp.cos(angles), jnp.sin(angles)
        cosv = jnp.concatenate([cos_a, cos_a], axis=1)
        sinv = jnp.concatenate([-sin_a, sin_a], axis=1)
        q, kn, vn = qkv(x_tok, g_attn.astype(F32)[None, :], cosv, sinv, wq, wk, wv)
        shape = (batch, 8, 16, 128)
        k_out, v_out, att = attn(seq_lens, q, kn, vn, k_blk.reshape(shape), v_blk.reshape(shape))
        y = tail(att, x_tok, g_mlp.astype(F32)[None, :], wo, wg, wu, wd)
        return y, k_out.reshape(k_blk.shape), v_out.reshape(v_blk.shape)

    return jax.shard_map(local_step, mesh=mesh, in_specs=(full_spec, full_spec, cache_spec, cache_spec, full_spec, col_spec, col_spec, col_spec, row_spec, full_spec, col_spec, col_spec, row_spec), out_specs=(full_spec, cache_spec, cache_spec), check_vma=False)
```

time: 524 us -> 162 us (0.31)
  waiting for transfers between devices: 368 us -> 0 us
  Pallas kernels: 0 us -> 151 us
  matrix products: 76.6 us -> 0 us
  other arithmetic: 44.7 us -> 4.66 us
  between operations: 14 us -> 0.66 us
  blocking collectives: 13 us -> 0 us
    psum x3 -> x0, waiting for transfers between devices: 368 us -> none  [the longest x1 153 us: local_step(): lax.psum(jnp.dot(attn_out, wo_loc, preferred_element_type=jnp.float32), '...]
    pallas_call x0 -> x3, Pallas kernels: none -> 151 us  [the longest x1 96 us: tail(): pl.pallas_call(tail_kernel, out_shape=jax.ShapeDtypeStruct((batch, dim),...]
    dot_general x8 -> x0, matrix products: 76.6 us -> none  [the longest x1 30.3 us: local_step(): jnp.dot(act_prod, wd_loc, preferred_element_type=jnp.float32)]
    select_n x1 -> x0, other arithmetic: 26.6 us -> none  [local_step(): v_out = jnp.where(is_new, v_new[:, None], v_blk)]
    pmax x1 -> x0, blocking collectives: 13 us -> none  [local_step(): glob_max = lax.pmax(blk_max, 'sp')]
    convert_element_type x6 -> x1, other arithmetic: 8.06 us -> 0.68 us  [local_step(): angles = seq_lens.astype(F32)[:, None] * inv_freq]
    reduce_sum x3 -> x0, other arithmetic: 6.54 us -> none  [the longest x2 5.1 us: rms_norm(): jnp.mean(x_f32 * x_f32, axis=-1, keepdims=True) + NORM_EPS]
  transfers between devices with their start and end apart: 3 -> 0, of which waited for: 3 -> 0; matrix products, arithmetic and copies ran while one was open for 0% -> 0% of each run, Pallas kernels for 0% -> 0%
where the time goes in v1:
time: 162 us; the launch traced here: 159 us
  Pallas kernels  151 us (93%)
  other arithmetic  4.66 us (3%)
  local copies, waits for them, and re-layouts  3.13 us (2%)
    pallas_call x1, Pallas kernels, tail(): pl.pallas_call(tail_kernel, out_shape=jax.ShapeDtypeStruct((batch, dim),...  96 us
    pallas_call x1, Pallas kernels, attn(): pl.pallas_call(attn_kernel, grid_spec=pltpu.PrefetchScalarGridSpec(num_sc...  38.1 us
    pallas_call x1, Pallas kernels, qkv(): pl.pallas_call(qkv_kernel, out_shape=(jax.ShapeDtypeStruct((rows * heads,...  16.7 us

profile of v1, /device:TPU:1, one launch (start us, length us, event | category | flops | bytes accessed | tf_op | source)
XLA Modules:
  0.0 159.3 jit_solution(13926364372726810862)
XLA Ops:
  0.6 0.7 convert_element_type.2
  1.3 1.3 broadcast_in_dim.16
  2.6 1.3 broadcast_in_dim.17
  3.9 0.5 fusion
  4.5 0.8 pad_maximum_fusion
  5.3 16.7 %qkv.1 = (f32[2048,128]{1,0:T(8,128)}, f32[512,128]{1,0:T(8,128)}, f32[512,128]{1,0:T(8,128)}) custom-call(bf16[256,4096]{1,0:T(8,128)(2,1)} %x_hbm.3, f32[1,4096]{1,0:T(1,128)} %bitcast.9, f32[256,128]{1,0:T(8,128)} %get-tuple-element.18.cos_ref, f32[256,128]{1,0:T(8,128)} %get-tuple-element.19.sin_ref, bf16[4096,1024]{1,0:T(8,128)(2,1)} %wq_hbm.1, ...), custom_call_target="tpu_custom_call" | custom-call | flops 3221225472 | bytes 12582912 | tf_op jit(solution)/shard_map/qkv/pallas_call | solution.py:68
  22.0 38.1 %attn.1 = (bf16[256,8,16,128]{3,2,1,0:T(8,128)(2,1)}, bf16[256,8,16,128]{3,2,1,0:T(8,128)(2,1)}, f32[8,272,128]{2,1,0:T(8,128)}) custom-call(s32[256]{0:T(256)} %lens_ref.1, f32[2048,128]{1,0:T(8,128)} %get-tuple-element.9.q_ref, f32[512,128]{1,0:T(8,128)} %get-tuple-element.10.kn_ref, f32[512,128]{1,0:T(8,128)} %get-tuple-element.11.vn_ref, ...), custom_call_target="tpu_custom_call" | custom-call | flops 268435456 | bytes 33554432 | tf_op jit(solution)/shard_map/attn/pallas_call | solution.py:150
  60.1 96.0 %tail.1 = bf16[256,4096]{1,0:T(8,128)(2,1)} custom-call(f32[8,272,128]{2,1,0:T(8,128)} %get-tuple-element.12.att_ref, bf16[256,4096]{1,0:T(8,128)(2,1)} %x_hbm.3, f32[1,4096]{1,0:T(1,128)} %bitcast.8, bf16[1024,4096]{1,0:T(8,128)(2,1)} %wo_hbm.1, bf16[4096,3584]{1,0:T(8,128)(2,1)} %wg_hbm.1, bf16[4096,3584]{1,0:T(8,128)(2,1)} %wu_hbm.1, ...), custom_call_target="tpu_custom_call" | custom-call | flops 2818572288 | bytes 44040192 | tf_op jit(solution)/shard_map/tail/pallas_call | solution.py:390
  156.2 3.1 %copy.17 = bf16[256,4096]{1,0:T(8,128)(2,1)} copy(bf16[256,4096]{1,0:T(8,128)(2,1)} %tail.1) | data formatting | bytes 4194304
  (1 shorter events, 0.0 us)

commit v2 on v1

--- a/solution.py
+++ b/solution.py
@@ -2,6 +2,7 @@
 
 import jax
 import jax.numpy as jnp
+import numpy as np
 from jax import lax
 from jax.experimental import pallas as pl
 from jax.experimental.pallas import tpu as pltpu
@@ -18,18 +19,46 @@
 BLK = 256
 
 
-def qkv_kernel(x_hbm, g_ref, cos_ref, sin_ref, wq_hbm, wk_hbm, wv_hbm, q_ref, k_ref, v_ref, x_buf, u_buf, w_buf, x_sem, w_sem):
-    rows = x_buf.shape[0]
-    dim = x_buf.shape[1]
-    nq = wq_hbm.shape[1] // BLK
+def front_kernel(
+    lens_ref, x_hbm, g_ref, cos_ref, sin_ref, wq_hbm, wk_hbm, wv_hbm, k_hbm, v_hbm, ko_hbm, vo_hbm, out_ref,
+    x_buf, u_buf, w_buf, k_buf, v_buf, q_buf, kn_buf, vn_buf, xsem, wsem, kvsem, osem,
+):
+    rows, dim = x_buf.shape
+    wide = 2 * BLK
+    nq = wq_hbm.shape[1] // wide
     heads = wq_hbm.shape[1] // 128
-    copies = [pltpu.make_async_copy(wq_hbm.at[:, pl.ds(i * BLK, BLK)], w_buf.at[i], w_sem.at[i]) for i in range(nq)]
-    copies.append(pltpu.make_async_copy(wk_hbm, w_buf.at[nq], w_sem.at[nq]))
-    copies.append(pltpu.make_async_copy(wv_hbm, w_buf.at[nq + 1], w_sem.at[nq + 1]))
-    x_copy = pltpu.make_async_copy(x_hbm, x_buf, x_sem)
+    nreq = 32
+    groups = rows // nreq
+    base = lax.axis_index("sp") * 64
+
+    x_copy = pltpu.make_async_copy(x_hbm, x_buf, xsem)
     x_copy.start()
-    for cp in copies:
-        cp.start()
+    w_copies = [[pltpu.make_async_copy(wq_hbm.at[:, pl.ds(i * wide, wide)], w_buf.at[i], wsem.at[i])] for i in range(nq)]
+    w_copies.append([
+        pltpu.make_async_copy(wk_hbm, w_buf.at[nq, :, pl.ds(0, BLK)], wsem.at[nq]),
+        pltpu.make_async_copy(wv_hbm, w_buf.at[nq, :, pl.ds(BLK, BLK)], wsem.at[nq + 1]),
+    ])
+    for cps in w_copies:
+        for cp in cps:
+            cp.start()
+
+    def cache_copies(g):
+        at = pl.ds(g * nreq, nreq)
+        return (
+            pltpu.make_async_copy(k_hbm.at[at], k_buf.at[at], kvsem.at[0, g]),
+            pltpu.make_async_copy(v_hbm.at[at], v_buf.at[at], kvsem.at[1, g]),
+        )
+
+    def out_copies(g):
+        at = pl.ds(g * nreq, nreq)
+        return (
+            pltpu.make_async_copy(k_buf.at[at], ko_hbm.at[at], osem.at[0, g]),
+            pltpu.make_async_copy(v_buf.at[at], vo_hbm.at[at], osem.at[1, g]),
+        )
+
+    for g in range(groups):
+        for cp in cache_copies(g):
+            cp.start()
     x_copy.wait()
     gain = g_ref[...]
 
@@ -48,128 +77,122 @@
         h = h.astype(BF16).astype(F32)
         return (h * cosv + pltpu.roll(h, 64, 1) * sinv).astype(BF16).astype(F32)
 
-    for i in range(nq + 2):
-        copies[i].wait()
+    for i in range(nq + 1):
+        for cp in w_copies[i]:
+            cp.wait()
         prod = jnp.dot(u_buf[...], w_buf[i], preferred_element_type=F32)
-        for s in range(2):
+        for s in range(4):
             part = prod[:, s * 128 : (s + 1) * 128]
             if i < nq:
-                q_ref[pl.ds(2 * i + s, rows, stride=heads), :] = rope(part)
-            elif i == nq:
-                k_ref[pl.ds(s, rows, stride=2), :] = rope(part)
+                q_buf[pl.ds(4 * i + s, rows, stride=heads), :] = rope(part)
+            elif s < 2:
+                kn_buf[pl.ds(s, rows, stride=2), :] = rope(part)
             else:
-                v_ref[pl.ds(s, rows, stride=2), :] = part.astype(BF16).astype(F32)
-
-
-def qkv(x, g, cosv, sinv, wq, wk, wv):
-    rows, dim = x.shape
-    heads = wq.shape[1] // 128
-    nblk = wq.shape[1] // BLK + 2
-    return pl.pallas_call(
-        qkv_kernel,
-        out_shape=(
-            jax.ShapeDtypeStruct((rows * heads, 128), F32),
-            jax.ShapeDtypeStruct((rows * 2, 128), F32),
-            jax.ShapeDtypeStruct((rows * 2, 128), F32),
-        ),
-        in_specs=[ANY, VMEM, VMEM, VMEM, ANY, ANY, ANY],
-        out_specs=(VMEM, VMEM, VMEM),
-        scratch_shapes=[
-            pltpu.VMEM((rows, dim), BF16),
-            pltpu.VMEM((rows, dim), BF16),
-            pltpu.VMEM((nblk, dim, BLK), BF16),
-            pltpu.SemaphoreType.DMA,
-            pltpu.SemaphoreType.DMA((nblk,)),
-        ],
-        compiler_params=pltpu.CompilerParams(vmem_limit_bytes=63_000_000),
-        cost_estimate=pl.CostEstimate(flops=2 * rows * dim * nblk * BLK, bytes_accessed=2 * dim * nblk * BLK, transcendentals=0),
-        name="qkv",
-    )(x, g, cosv, sinv, wq, wk, wv)
-
-
-def attn_kernel(lens_ref, q_ref, kn_ref, vn_ref, k_ref, v_ref, ko_ref, vo_ref, out_ref):
-    nreq = k_ref.shape[0]
-    base = lax.axis_index("sp") * 64
-    g = pl.program_id(0)
+                vn_buf[pl.ds(s - 2, rows, stride=2), :] = part.astype(BF16).astype(F32)
+
     lane = lax.broadcasted_iota(jnp.int32, (8, 128), 1)
     head = lax.broadcasted_iota(jnp.int32, (8, 128), 0)
     match = (lane % 2) == (head // 4)
     lane_pos = jnp.where(match, lane // 2, 1 << 20)
-    row_pos = (lax.broadcasted_iota(jnp.int32, (8, 16, 128), 0) * 8 + lax.broadcasted_iota(jnp.int32, (8, 16, 128), 1) // 2).astype(F32).astype(BF16)
-    odd = (lax.broadcasted_iota(jnp.int32, (16, 128), 0) % 2) == 1
+    row16 = lax.broadcasted_iota(jnp.int32, (16, 128), 0)
     scale = 128.0**-0.5
     zero = jnp.zeros((8, 128), BF16)
 
-    def update(c_ref, n_ref, o_ref, b, pos_b):
-        row0 = jnp.broadcast_to(n_ref[pl.ds(2 * b, 1), :], (16, 128))
-        row1 = jnp.broadcast_to(n_ref[pl.ds(2 * b + 1, 1), :], (16, 128))
-        new = jnp.where(odd, row1, row0).astype(BF16)
-        upd = jnp.where(row_pos == pos_b, new[None], c_ref[b])
-        o_ref[b] = upd
-        return upd.reshape(128, 128)
-
-    def step(it, carry):
-        stm, stl = carry
-        for pair in range(4):
-            keys, vals, poss = [], [], []
-            first = it * 8 + pair * 2
-            for j in range(2):
-                b = first + j
-                pos = lens_ref[g * nreq + b] - base
-                pos_b = jnp.full((8, 16, 128), pos, jnp.int32).astype(F32).astype(BF16)
-                keys.append(update(k_ref, kn_ref, ko_ref, b, pos_b))
-                vals.append(update(v_ref, vn_ref, vo_ref, b, pos_b))
-                poss.append(pos)
-            qrow = pl.multiple_of(first * 8, 16)
-            qp = q_ref[pl.ds(qrow, 16), :].astype(BF16)
-            sc = lax.dot_general(qp, jnp.concatenate(keys, axis=0), (((1,), (1,)), ((), ())), preferred_element_type=F32) * scale
+    def insert(b, c_buf, n_buf, blk, off):
+        row0 = jnp.broadcast_to(n_buf[pl.ds(2 * b, 1), :], (16, 128))
+        row1 = jnp.broadcast_to(n_buf[pl.ds(2 * b + 1, 1), :], (16, 128))
+        new = jnp.where(row16 == off, row0, row1)
+        old = c_buf[b, blk].astype(F32)
+        c_buf[b, blk] = jnp.where((row16 == off) | (row16 == off + 1), new, old).astype(BF16)
+
+    def group(g, carry):
+        for cp in cache_copies(g):
+            cp.wait()
+
+        def put(i, c):
+            b = g * nreq + i
+            pos = lens_ref[b] - base
+            inside = (pos >= 0) & (pos < 64)
+            at = jnp.where(inside, pos, 0)
+            off = jnp.where(inside, 2 * (at % 8), -8)
+            insert(b, k_buf, kn_buf, at // 8, off)
+            insert(b, v_buf, vn_buf, at // 8, off)
+            return c
+
+        lax.fori_loop(0, nreq, put, 0, unroll=4)
+        for cp in out_copies(g):
+            cp.start()
+
+        def step(it, c):
+            stm, stl = c
+            first = g * nreq + it * 16
+            scores = []
+            for p in range(8):
+                b = first + 2 * p
+                keys = k_buf[pl.ds(b, 2)].reshape(256, 128)
+                qp = q_buf[pl.ds(pl.multiple_of(b * 8, 16), 16), :].astype(BF16)
+                scores.append(lax.dot_general(qp, keys, (((1,), (1,)), ((), ())), preferred_element_type=F32))
             wts = []
-            for j in range(2):
-                s = sc[8 * j : 8 * j + 8, 128 * j : 128 * j + 128]
-                valid = lane_pos <= poss[j]
-                m = jnp.max(jnp.where(valid, s, NEG), axis=1, keepdims=True)
-                w = jnp.where(valid, jnp.exp(s - m), 0.0)
-                here = lane == first + j
-                stm = jnp.where(here, m, stm)
-                stl = jnp.where(here, jnp.sum(w, axis=1, keepdims=True), stl)
-                wts.append(w.astype(BF16))
-            wp = jnp.concatenate([jnp.concatenate([wts[0], zero], axis=1), jnp.concatenate([zero, wts[1]], axis=1)], axis=0)
-            out_ref[0, pl.ds(qrow, 16), :] = jnp.dot(wp, jnp.concatenate(vals, axis=0), preferred_element_type=F32)
-        return stm, stl
-
-    stm, stl = lax.fori_loop(0, nreq // 8, step, (jnp.zeros((8, 128), F32), jnp.ones((8, 128), F32)))
-    out_ref[0, pl.ds(nreq * 8, 8), :] = stm
-    out_ref[0, pl.ds(nreq * 8 + 8, 8), :] = stl
-
-
-def attn(lens, q, kn, vn, k, v):
-    batch = k.shape[0]
-    nreq = 32
-    steps = batch // nreq
-    cache = pl.BlockSpec((nreq, 8, 16, 128), lambda i, *_: (i, 0, 0, 0))
+            for p in range(8):
+                for j in range(2):
+                    s = scores[p][8 * j : 8 * j + 8, 128 * j : 128 * j + 128] * scale
+                    valid = lane_pos <= lens_ref[first + 2 * p + j] - base
+                    m = jnp.max(jnp.where(valid, s, NEG), axis=1, keepdims=True)
+                    w = jnp.where(valid, jnp.exp(s - m), 0.0)
+                    here = lane == it * 16 + 2 * p + j
+                    stm = jnp.where(here, m, stm)
+                    stl = jnp.where(here, jnp.sum(w, axis=1, keepdims=True), stl)
+                    wts.append(w.astype(BF16))
+            for p in range(8):
+                wp = jnp.concatenate([jnp.concatenate([wts[2 * p], zero], axis=1), jnp.concatenate([zero, wts[2 * p + 1]], axis=1)], axis=0)
+                vals = v_buf[pl.ds(first + 2 * p, 2)].reshape(256, 128)
+                out_ref[g, pl.ds(pl.multiple_of(it * 128 + p * 16, 16), 16), :] = jnp.dot(wp, vals, preferred_element_type=F32)
+            return stm, stl
+
+        stm, stl = lax.fori_loop(0, nreq // 16, step, (jnp.zeros((8, 128), F32), jnp.ones((8, 128), F32)))
+        out_ref[g, pl.ds(nreq * 8, 8), :] = stm
+        out_ref[g, pl.ds(nreq * 8 + 8, 8), :] = stl
+        return carry
+
+    lax.fori_loop(0, groups, group, 0)
+    for g in range(groups):
+        for cp in out_copies(g):
+            cp.wait()
+
+
+def front(lens, x, g, cosv, sinv, wq, wk, wv, k, v):
+    rows, dim = x.shape
+    heads = wq.shape[1] // 128
+    nblk = wq.shape[1] // (2 * BLK) + 1
+    groups = rows // 32
+    dma = pltpu.SemaphoreType.DMA
     return pl.pallas_call(
-        attn_kernel,
-        grid_spec=pltpu.PrefetchScalarGridSpec(
-            num_scalar_prefetch=1,
-            grid=(steps,),
-            in_specs=[
-                pl.BlockSpec((nreq * 8, 128), lambda i, *_: (i, 0)),
-                pl.BlockSpec((nreq * 2, 128), lambda i, *_: (i, 0)),
-                pl.BlockSpec((nreq * 2, 128), lambda i, *_: (i, 0)),
-                cache,
-                cache,
-            ],
-            out_specs=[cache, cache, pl.BlockSpec((1, nreq * 8 + 16, 128), lambda i, *_: (i, 0, 0))],
-        ),
-        out_shape=[
+        front_kernel,
+        out_shape=(
             jax.ShapeDtypeStruct(k.shape, BF16),
             jax.ShapeDtypeStruct(v.shape, BF16),
-            jax.ShapeDtypeStruct((steps, nreq * 8 + 16, 128), F32),
+            jax.ShapeDtypeStruct((groups, 32 * 8 + 16, 128), F32),
+        ),
+        in_specs=[pl.BlockSpec(memory_space=pltpu.SMEM), ANY, VMEM, VMEM, VMEM, ANY, ANY, ANY, ANY, ANY],
+        out_specs=(ANY, ANY, VMEM),
+        scratch_shapes=[
+            pltpu.VMEM((rows, dim), BF16),
+            pltpu.VMEM((rows, dim), BF16),
+            pltpu.VMEM((nblk, dim, 2 * BLK), BF16),
+            pltpu.VMEM(k.shape, BF16),
+            pltpu.VMEM(v.shape, BF16),
+            pltpu.VMEM((rows * heads, 128), F32),
+            pltpu.VMEM((rows * 2, 128), F32),
+            pltpu.VMEM((rows * 2, 128), F32),
+            dma,
+            dma((nblk + 1,)),
+            dma((2, groups)),
+            dma((2, groups)),
         ],
-        compiler_params=pltpu.CompilerParams(vmem_limit_bytes=63_000_000, dimension_semantics=("arbitrary",)),
-        cost_estimate=pl.CostEstimate(flops=batch * 2**20, bytes_accessed=8 * k.size, transcendentals=0),
-        name="attn",
-    )(lens, q, kn, vn, k, v)
+        compiler_params=pltpu.CompilerParams(vmem_limit_bytes=63_000_000),
+        cost_estimate=pl.CostEstimate(flops=4 * rows * dim * nblk * BLK, bytes_accessed=4 * dim * nblk * BLK + 8 * k.size, transcendentals=0),
+        name="front",
+    )(lens, x, g, cosv, sinv, wq, wk, wv, k, v)
 
 
 def merge(blocks, out_ref, rows, last):
@@ -432,14 +455,11 @@
 
     def local_step(x_tok, seq_lens, k_blk, v_blk, g_attn, wq, wk, wv, wo, g_mlp, wg, wu, wd):
         batch = x_tok.shape[0]
-        inv_freq = jnp.power(jnp.float32(ROPE_BASE), jnp.arange(64, dtype=F32) * (-2.0 / 128))
-        angles = seq_lens.astype(F32)[:, None] * inv_freq
-        cos_a, sin_a = jnp.cos(angles), jnp.sin(angles)
-        cosv = jnp.concatenate([cos_a, cos_a], axis=1)
-        sinv = jnp.concatenate([-sin_a, sin_a], axis=1)
-        q, kn, vn = qkv(x_tok, g_attn.astype(F32)[None, :], cosv, sinv, wq, wk, wv)
+        freq = np.power(np.float32(ROPE_BASE), np.arange(64, dtype=np.float32) * np.float32(-2.0 / 128))
+        angles = seq_lens.astype(F32)[:, None] * jnp.asarray(np.concatenate([freq, freq])[None, :], F32)
+        sign = jnp.asarray(np.concatenate([-np.ones(64), np.ones(64)])[None, :], F32)
         shape = (batch, 8, 16, 128)
-        k_out, v_out, att = attn(seq_lens, q, kn, vn, k_blk.reshape(shape), v_blk.reshape(shape))
+        k_out, v_out, att = front(seq_lens, x_tok, g_attn.astype(F32)[None, :], jnp.cos(angles), jnp.sin(angles) * sign, wq, wk, wv, k_blk.reshape(shape), v_blk.reshape(shape))
         y = tail(att, x_tok, g_mlp.astype(F32)[None, :], wo, wg, wu, wd)
         return y, k_out.reshape(k_blk.shape), v_out.reshape(v_blk.shape)
 

time: 162 us -> 136 us (0.84)
  Pallas kernels: 151 us -> 125 us
    pallas_call x2 -> x1, Pallas kernels: 54.8 us -> 28.5 us  [front(): pl.pallas_call(front_kernel, out_shape=(jax.ShapeDtypeStruct(k.shape, BF1...]
    mul x0 -> x1, other arithmetic: none -> 1.91 us  [local_step(): jnp.sin(angles) * sign]
where the time goes in v2:
time: 136 us; the launch traced here: 134 us
  Pallas kernels  125 us (92%)
  other arithmetic  5.19 us (4%)
  local copies, waits for them, and re-layouts  3.13 us (2%)
    pallas_call x1, Pallas kernels, tail(): pl.pallas_call(tail_kernel, out_shape=jax.ShapeDtypeStruct((batch, dim),...  96.2 us
    pallas_call x1, Pallas kernels, front(): pl.pallas_call(front_kernel, out_shape=(jax.ShapeDtypeStruct(k.shape, BF1...  28.5 us
    unnamed x1, local copies, waits for them, and re-layouts  3.13 us

profile of v2, /device:TPU:1, one launch (start us, length us, event | category | flops | bytes accessed | tf_op | source)
XLA Modules:
  0.0 133.6 jit_solution(4155516400729561555)
XLA Ops:
  0.6 0.7 convert_element_type.2
  1.3 1.3 broadcast_in_dim.15
  2.6 1.3 broadcast_in_dim.16
  3.9 1.9 %fusion = (f32[256,128]{1,0:T(8,128)}, f32[256,128]{1,0:T(8,128)}) fusion(f32[128]{0:T(128)} %constant.9, f32[128]{0:T(128)} %constant.8, f32[256]{0:T(256)S(1)} %convert_element_type.2), kind=kLoop, calls=%fused_computation.2 | loop fusion | flops 65536 | bytes 264192 | tf_op jit(solution)/shard_map/mul | solution.py:462
  5.8 28.5 %front.1 = (bf16[256,8,16,128]{3,2,1,0:T(8,128)(2,1)}, bf16[256,8,16,128]{3,2,1,0:T(8,128)(2,1)}, f32[8,272,128]{2,1,0:T(8,128)}) custom-call(s32[256]{0:T(256)} %lens_ref.1, bf16[256,4096]{1,0:T(8,128)(2,1)} %x_hbm.3, f32[1,4096]{1,0:T(1,128)} %bitcast.9, f32[256,128]{1,0:T(8,128)} %get-tuple-element.10.cos_ref, f32[256,128]{1,0:T(8,128)} %get-tuple-element.9.sin_ref, ...), custom_call_target="tpu_custom_call" | custom-call | flops 3221225472 | bytes 46137344 | tf_op jit(solution)/shard_map/front/pallas_call | solution.py:169
  34.3 96.2 %tail.1 = bf16[256,4096]{1,0:T(8,128)(2,1)} custom-call(f32[8,272,128]{2,1,0:T(8,128)} %get-tuple-element.6.att_ref, bf16[256,4096]{1,0:T(8,128)(2,1)} %x_hbm.3, f32[1,4096]{1,0:T(1,128)} %bitcast.8, bf16[1024,4096]{1,0:T(8,128)(2,1)} %wo_hbm.1, bf16[4096,3584]{1,0:T(8,128)(2,1)} %wg_hbm.1, bf16[4096,3584]{1,0:T(8,128)(2,1)} %wu_hbm.1, bf16[3584,4096]{1,0:T(8,128)(2,1)} %wd_hbm.1), custom_call_target="tpu_custom_call" | custom-call | flops 2818572288 | bytes 44040192 | tf_op jit(solution)/shard_map/tail/pallas_call | solution.py:413
  130.5 3.1 %copy.19 = bf16[256,4096]{1,0:T(8,128)(2,1)} copy(bf16[256,4096]{1,0:T(8,128)(2,1)} %tail.1) | data formatting | bytes 4194304

commit v3 on v2

--- a/solution.py
+++ b/solution.py
@@ -17,11 +17,12 @@
 VMEM = pl.BlockSpec(memory_space=pltpu.VMEM)
 NEG = -1e30
 BLK = 256
+PART = 144
 
 
 def front_kernel(
-    lens_ref, x_hbm, g_ref, cos_ref, sin_ref, wq_hbm, wk_hbm, wv_hbm, k_hbm, v_hbm, ko_hbm, vo_hbm, out_ref,
-    x_buf, u_buf, w_buf, k_buf, v_buf, q_buf, kn_buf, vn_buf, xsem, wsem, kvsem, osem,
+    lens_ref, x_hbm, g_hbm, tab_hbm, wq_hbm, wk_hbm, wv_hbm, k_hbm, v_hbm, ko_hbm, vo_hbm, out_hbm,
+    x_buf, g_buf, tab_buf, rot_buf, u_buf, w_buf, k_buf, v_buf, q_buf, kn_buf, vn_buf, out_buf, xsem, wsem, kvsem, osem,
 ):
     rows, dim = x_buf.shape
     wide = 2 * BLK
@@ -31,8 +32,12 @@
     groups = rows // nreq
     base = lax.axis_index("sp") * 64
 
-    x_copy = pltpu.make_async_copy(x_hbm, x_buf, xsem)
+    x_copy = pltpu.make_async_copy(x_hbm, x_buf, xsem.at[0])
+    g_copy = pltpu.make_async_copy(g_hbm, g_buf, xsem.at[1])
+    tab_copy = pltpu.make_async_copy(tab_hbm, tab_buf, xsem.at[2])
+    g_copy.start()
     x_copy.start()
+    tab_copy.start()
     w_copies = [[pltpu.make_async_copy(wq_hbm.at[:, pl.ds(i * wide, wide)], w_buf.at[i], wsem.at[i])] for i in range(nq)]
     w_copies.append([
         pltpu.make_async_copy(wk_hbm, w_buf.at[nq, :, pl.ds(0, BLK)], wsem.at[nq]),
@@ -56,11 +61,15 @@
             pltpu.make_async_copy(v_buf.at[at], vo_hbm.at[at], osem.at[1, g]),
         )
 
+    def part_copy(g):
+        return pltpu.make_async_copy(out_buf.at[pl.ds(2 * g, 2)], out_hbm.at[pl.ds(2 * g, 2)], osem.at[2, g])
+
     for g in range(groups):
         for cp in cache_copies(g):
             cp.start()
+    g_copy.wait()
+    gain = g_buf[...].astype(F32).reshape(1, dim)
     x_copy.wait()
-    gain = g_ref[...]
 
     def norm(i, carry):
         at = pl.ds(pl.multiple_of(i * 16, 16), 16)
@@ -69,9 +78,16 @@
         u_buf[at, :] = (xf * inv * gain).astype(BF16)
         return carry
 
-    lax.fori_loop(0, rows // 16, norm, 0)
-    cosv = cos_ref[...]
-    sinv = sin_ref[...]
+    lax.fori_loop(0, rows // 16, norm, 0, unroll=2)
+    tab_copy.wait()
+
+    def angle(i, carry):
+        rot_buf[pl.ds(i, 1), :] = tab_buf[pl.ds(lens_ref[i], 1), :]
+        return carry
+
+    lax.fori_loop(0, rows, angle, 0, unroll=16)
+    cosv = rot_buf[:, :128]
+    sinv = rot_buf[:, 128:]
 
     def rope(h):
         h = h.astype(BF16).astype(F32)
@@ -119,48 +135,48 @@
             insert(b, v_buf, vn_buf, at // 8, off)
             return c
 
-        lax.fori_loop(0, nreq, put, 0, unroll=4)
+        lax.fori_loop(0, nreq, put, 0, unroll=8)
         for cp in out_copies(g):
             cp.start()
 
-        def step(it, c):
-            stm, stl = c
-            first = g * nreq + it * 16
-            scores = []
-            for p in range(8):
-                b = first + 2 * p
-                keys = k_buf[pl.ds(b, 2)].reshape(256, 128)
-                qp = q_buf[pl.ds(pl.multiple_of(b * 8, 16), 16), :].astype(BF16)
-                scores.append(lax.dot_general(qp, keys, (((1,), (1,)), ((), ())), preferred_element_type=F32))
+        first = g * nreq
+        scores = []
+        for p in range(16):
+            b = first + 2 * p
+            keys = k_buf[pl.ds(b, 2)].reshape(256, 128)
+            qp = q_buf[pl.ds(pl.multiple_of(b * 8, 16), 16), :].astype(BF16)
+            scores.append(lax.dot_general(qp, keys, (((1,), (1,)), ((), ())), preferred_element_type=F32))
+        for h in range(2):
+            half = g * 2 + h
             wts = []
+            stm, stl = jnp.zeros((8, 128), F32), jnp.ones((8, 128), F32)
             for p in range(8):
                 for j in range(2):
-                    s = scores[p][8 * j : 8 * j + 8, 128 * j : 128 * j + 128] * scale
-                    valid = lane_pos <= lens_ref[first + 2 * p + j] - base
+                    s = scores[8 * h + p][8 * j : 8 * j + 8, 128 * j : 128 * j + 128] * scale
+                    valid = lane_pos <= lens_ref[first + 16 * h + 2 * p + j] - base
                     m = jnp.max(jnp.where(valid, s, NEG), axis=1, keepdims=True)
                     w = jnp.where(valid, jnp.exp(s - m), 0.0)
-                    here = lane == it * 16 + 2 * p + j
+                    here = lane == 2 * p + j
                     stm = jnp.where(here, m, stm)
                     stl = jnp.where(here, jnp.sum(w, axis=1, keepdims=True), stl)
                     wts.append(w.astype(BF16))
+            out_buf[half, 128:136, :] = stm
+            out_buf[half, 136:144, :] = stl
             for p in range(8):
                 wp = jnp.concatenate([jnp.concatenate([wts[2 * p], zero], axis=1), jnp.concatenate([zero, wts[2 * p + 1]], axis=1)], axis=0)
-                vals = v_buf[pl.ds(first + 2 * p, 2)].reshape(256, 128)
-                out_ref[g, pl.ds(pl.multiple_of(it * 128 + p * 16, 16), 16), :] = jnp.dot(wp, vals, preferred_element_type=F32)
-            return stm, stl
-
-        stm, stl = lax.fori_loop(0, nreq // 16, step, (jnp.zeros((8, 128), F32), jnp.ones((8, 128), F32)))
-        out_ref[g, pl.ds(nreq * 8, 8), :] = stm
-        out_ref[g, pl.ds(nreq * 8 + 8, 8), :] = stl
+                vals = v_buf[pl.ds(first + 16 * h + 2 * p, 2)].reshape(256, 128)
+                out_buf[half, 16 * p : 16 * p + 16, :] = jnp.dot(wp, vals, preferred_element_type=F32)
+        part_copy(g).start()
         return carry
 
     lax.fori_loop(0, groups, group, 0)
     for g in range(groups):
         for cp in out_copies(g):
             cp.wait()
-
-
-def front(lens, x, g, cosv, sinv, wq, wk, wv, k, v):
+        part_copy(g).wait()
+
+
+def front(lens, x, g, tab, wq, wk, wv, k, v):
     rows, dim = x.shape
     heads = wq.shape[1] // 128
     nblk = wq.shape[1] // (2 * BLK) + 1
@@ -171,12 +187,15 @@
         out_shape=(
             jax.ShapeDtypeStruct(k.shape, BF16),
             jax.ShapeDtypeStruct(v.shape, BF16),
-            jax.ShapeDtypeStruct((groups, 32 * 8 + 16, 128), F32),
+            jax.ShapeDtypeStruct((2 * groups, PART, 128), F32),
         ),
-        in_specs=[pl.BlockSpec(memory_space=pltpu.SMEM), ANY, VMEM, VMEM, VMEM, ANY, ANY, ANY, ANY, ANY],
-        out_specs=(ANY, ANY, VMEM),
+        in_specs=[pl.BlockSpec(memory_space=pltpu.SMEM)] + [ANY] * 8,
+        out_specs=(ANY, ANY, ANY),
         scratch_shapes=[
             pltpu.VMEM((rows, dim), BF16),
+            pltpu.VMEM((dim,), BF16),
+            pltpu.VMEM(tab.shape, F32),
+            pltpu.VMEM((rows, 256), F32),
             pltpu.VMEM((rows, dim), BF16),
             pltpu.VMEM((nblk, dim, 2 * BLK), BF16),
             pltpu.VMEM(k.shape, BF16),
@@ -184,18 +203,20 @@
             pltpu.VMEM((rows * heads, 128), F32),
             pltpu.VMEM((rows * 2, 128), F32),
             pltpu.VMEM((rows * 2, 128), F32),
-            dma,
+            pltpu.VMEM((2 * groups, PART, 128), F32),
+            dma((3,)),
             dma((nblk + 1,)),
             dma((2, groups)),
-            dma((2, groups)),
+            dma((3, groups)),
         ],
         compiler_params=pltpu.CompilerParams(vmem_limit_bytes=63_000_000),
         cost_estimate=pl.CostEstimate(flops=4 * rows * dim * nblk * BLK, bytes_accessed=4 * dim * nblk * BLK + 8 * k.size, transcendentals=0),
         name="front",
-    )(lens, x, g, cosv, sinv, wq, wk, wv, k, v)
-
-
-def merge(blocks, out_ref, rows, last):
+    )(lens, x, g, tab, wq, wk, wv, k, v)
+
+
+def merge(blocks, out_ref, last):
+    rows = PART - 16
     maxs = [b[rows : rows + 8, :] for b in blocks]
     top = functools.reduce(jnp.maximum, maxs)
     facs = [jnp.exp(m - top) for m in maxs]
@@ -225,7 +246,6 @@
     plane_id = [{"tp": tp, "sp": 2 * q + core} for q in plane]
     zs = [(tp + k) % 4 for k in range(4)]
     z_id = [{"tp": z, "sp": sp} for z in zs]
-    rows = att_ref.shape[1] - 16
     dim = x_buf.shape[1]
     ring = wg_buf.shape[0]
     half = wd_buf.shape[1]
@@ -268,19 +288,20 @@
         return cp
 
     order = [1, 2, 3, 0]
-    d1 = {k: send(att_ref.at[2 * plane[k] + (1 - core)], d1_buf.at[k], d1s.at[k], d1r.at[k], mate) for k in order}
+    d1 = {k: send(att_ref.at[pl.ds(4 * plane[k] + 2 * (1 - core), 2)], d1_buf.at[k], d1s.at[k], d1r.at[k], mate) for k in order}
     r1 = {}
     for k in order:
         d1[k].wait_recv()
-        merge([att_ref.at[2 * plane[k] + core], d1_buf.at[k]], m_buf.at[k], rows, False)
+        for h in range(2):
+            merge([att_ref.at[4 * plane[k] + 2 * core + h], d1_buf.at[k, h]], m_buf.at[k, h], False)
         if k:
             r1[k] = send(m_buf.at[k], r1_buf.at[k - 1], r1s.at[k - 1], r1r.at[k - 1], plane_id[k])
     for k in (1, 2, 3):
         r1[k].wait_recv()
-    merge([m_buf.at[0]] + [r1_buf.at[k] for k in range(3)], o_buf, rows, True)
-
-    nreq = rows // 8
-    o = jnp.concatenate([o_buf[pl.ds(h, nreq, stride=8), :].astype(BF16) for h in range(8)], axis=1)
+    for h in range(2):
+        merge([m_buf.at[0, h]] + [r1_buf.at[k, h] for k in range(3)], o_buf.at[pl.ds(128 * h, 128)], True)
+
+    o = jnp.concatenate([o_buf[pl.ds(h, 32, stride=8), :].astype(BF16) for h in range(8)], axis=1)
     wo_copy.wait()
 
     def proj(j, carry):
@@ -302,7 +323,7 @@
     hid_buf[...] = hid
     inv = lax.rsqrt(jnp.sum(hid * hid, axis=-1, keepdims=True) * (1.0 / dim) + NORM_EPS)
     mine = core * 4
-    h_buf[mine + tp] = (hid * inv * g_ref[...]).astype(BF16).astype(F32)
+    h_buf[mine + tp] = (hid * inv * g_ref[...].astype(F32).reshape(1, dim)).astype(BF16).astype(F32)
 
     hz = [send(h_buf.at[mine + tp], h_buf.at[mine + tp], hs.at[k - 1], hr.at[k - 1], z_id[k]) for k in (1, 2, 3)]
     hd = [send(h_buf.at[mine + tp], h_buf.at[mine + tp], hds.at[0], hdr.at[0], mate)]
@@ -405,7 +426,6 @@
 
 def tail(att, x, g, wo, wg, wu, wd):
     batch, dim = x.shape
-    groups, rows16, _ = att.shape
     half = wg.shape[1] // 2
     ring = min(4, half // BLK)
     ndn = 8
@@ -416,10 +436,10 @@
         in_specs=[VMEM, ANY, VMEM, ANY, ANY, ANY, ANY],
         out_specs=VMEM,
         scratch_shapes=[
-            pltpu.VMEM((4, rows16, 128), F32),
-            pltpu.VMEM((4, rows16, 128), F32),
-            pltpu.VMEM((3, rows16, 128), F32),
-            pltpu.VMEM((rows16 - 16, 128), F32),
+            pltpu.VMEM((4, 2, PART, 128), F32),
+            pltpu.VMEM((4, 2, PART, 128), F32),
+            pltpu.VMEM((3, 2, PART, 128), F32),
+            pltpu.VMEM((256, 128), F32),
             pltpu.VMEM((32, dim), F32),
             pltpu.VMEM((3, 8, dim), F32),
             pltpu.VMEM((8, 8, dim), F32),
@@ -447,6 +467,13 @@
     )(att, x, g, wo, wg, wu, wd)
 
 
+def rope_table(length):
+    freq = np.power(ROPE_BASE, np.arange(64) * (-2.0 / 128)).astype(np.float32)
+    angles = (np.arange(length, dtype=np.float32)[:, None] * freq).astype(np.float64)
+    cos, sin = np.cos(angles), np.sin(angles)
+    return jnp.asarray(np.concatenate([cos, cos, -sin, sin], axis=1), F32)
+
+
 def solution(mesh):
     cache_spec = P(None, "sp", "tp", None)
     col_spec = P(None, "tp")
@@ -455,12 +482,9 @@
 
     def local_step(x_tok, seq_lens, k_blk, v_blk, g_attn, wq, wk, wv, wo, g_mlp, wg, wu, wd):
         batch = x_tok.shape[0]
-        freq = np.power(np.float32(ROPE_BASE), np.arange(64, dtype=np.float32) * np.float32(-2.0 / 128))
-        angles = seq_lens.astype(F32)[:, None] * jnp.asarray(np.concatenate([freq, freq])[None, :], F32)
-        sign = jnp.asarray(np.concatenate([-np.ones(64), np.ones(64)])[None, :], F32)
         shape = (batch, 8, 16, 128)
-        k_out, v_out, att = front(seq_lens, x_tok, g_attn.astype(F32)[None, :], jnp.cos(angles), jnp.sin(angles) * sign, wq, wk, wv, k_blk.reshape(shape), v_blk.reshape(shape))
-        y = tail(att, x_tok, g_mlp.astype(F32)[None, :], wo, wg, wu, wd)
+        k_out, v_out, att = front(seq_lens, x_tok, g_attn, rope_table(k_blk.shape[1] * mesh.shape["sp"]), wq, wk, wv, k_blk.reshape(shape), v_blk.reshape(shape))
+        y = tail(att, x_tok, g_mlp, wo, wg, wu, wd)
         return y, k_out.reshape(k_blk.shape), v_out.reshape(v_blk.shape)
 
     return jax.shard_map(local_step, mesh=mesh, in_specs=(full_spec, full_spec, cache_spec, cache_spec, full_spec, col_spec, col_spec, col_spec, row_spec, full_spec, col_spec, col_spec, row_spec), out_specs=(full_spec, cache_spec, cache_spec), check_vma=False)

time: 136 us -> 127 us (0.934)
  the two profiles are of different devices: /device:TPU:1 before, /device:TPU:19 now
where the time goes in v3:
time: 127 us
  Pallas kernels  123 us (97%)
  local copies, waits for them, and re-layouts  3.13 us (2%)
    pallas_call x1, Pallas kernels, tail(): pl.pallas_call(tail_kernel, out_shape=jax.ShapeDtypeStruct((batch, dim),...  98.9 us
    pallas_call x1, Pallas kernels, front(): pl.pallas_call(front_kernel, out_shape=(jax.ShapeDtypeStruct(k.shape, BF1...  24.1 us
    unnamed x1, local copies, waits for them, and re-layouts  3.13 us

profile of v3, /device:TPU:19, one launch (start us, length us, event | category | flops | bytes accessed | tf_op | source)
XLA Modules:
  0.0 126.8 jit_solution(9306652994768778453)
XLA Ops:
  0.6 24.1 %front.1 = (bf16[256,8,16,128]{3,2,1,0:T(8,128)(2,1)}, bf16[256,8,16,128]{3,2,1,0:T(8,128)(2,1)}, f32[16,144,128]{2,1,0:T(8,128)}) custom-call(s32[256]{0:T(256)} %lens_ref.1, bf16[256,4096]{1,0:T(8,128)(2,1)} %x_hbm.3, bf16[4096]{0:T(1024)(128)(2,1)} %g_hbm.1, f32[512,256]{1,0:T(8,128)} %constant.2.clone.tab_hbm, bf16[4096,1024]{1,0:T(8,128)(2,1)} %wq_hbm.1, ...), custom_call_target="tpu_custom_call" | custom-call | flops 3221225472 | bytes 46137344 | tf_op jit(solution)/shard_map/front/pallas_call | solution.py:185
  24.7 98.9 %tail.1 = bf16[256,4096]{1,0:T(8,128)(2,1)} custom-call(f32[16,144,128]{2,1,0:T(8,128)} %get-tuple-element.6.att_ref, bf16[256,4096]{1,0:T(8,128)(2,1)} %x_hbm.3, bf16[4096]{0:T(1024)(128)(2,1)} %g_ref.1, bf16[1024,4096]{1,0:T(8,128)(2,1)} %wo_hbm.1, bf16[4096,3584]{1,0:T(8,128)(2,1)} %wg_hbm.1, bf16[4096,3584]{1,0:T(8,128)(2,1)} %wu_hbm.1, ...), custom_call_target="tpu_custom_call" | custom-call | flops 2818572288 | bytes 44040192 | tf_op jit(solution)/shard_map/tail/pallas_call | solution.py:433
  123.6 3.1 %copy.18 = bf16[256,4096]{1,0:T(8,128)(2,1)} copy(bf16[256,4096]{1,0:T(8,128)(2,1)} %tail.1) | data formatting | bytes 4194304

commit v4 on v3

--- a/solution.py
+++ b/solution.py
@@ -17,6 +17,7 @@
 VMEM = pl.BlockSpec(memory_space=pltpu.VMEM)
 NEG = -1e30
 BLK = 256
+CHUNKS = 4
 PART = 144
 
 
@@ -233,10 +234,10 @@
 
 
 def tail_kernel(
-    att_ref, x_hbm, g_ref, wo_hbm, wg_hbm, wu_hbm, wd_hbm, y_ref,
-    d1_buf, m_buf, r1_buf, o_buf, p_buf, z1_buf, h_buf, hb_buf, a_buf, p2_buf, d2_buf, s2_buf, z2_buf, yg_buf, x_buf, hid_buf,
+    att_ref, x_hbm, g_ref, wo_hbm, wg_hbm, wu_hbm, wd_hbm, y_hbm,
+    d1_buf, m_buf, r1_buf, o_buf, p_buf, z1_buf, a1_buf, h_buf, hb_buf, a_buf, p2_buf, d2_buf, s2_buf, z2_buf, a2_buf, yg_buf, yo_buf, x_buf, hid_buf,
     wo_buf, wg_buf, wu_buf, wd_buf,
-    lsem, gsem, usem, dsem, d1s, d1r, r1s, r1r, z1s, z1r, hs, hr, hds, hdr, d2s, d2r, z2s, z2r, ys, yr, ydr,
+    lsem, gsem, usem, dsem, osem, d1s, d1r, r1s, r1r, z1s, z1r, hs, hr, hds, hdr, d2s, d2r, z2s, z2r, ys, yr, ydr,
 ):
     tp, sp = lax.axis_index("tp"), lax.axis_index("sp")
     core, chip = sp % 2, sp // 2
@@ -244,8 +245,18 @@
     mate = {"tp": tp, "sp": 2 * chip + (1 - core)}
     plane = [(chip + k) % 4 for k in range(4)]
     plane_id = [{"tp": tp, "sp": 2 * q + core} for q in plane]
-    zs = [(tp + k) % 4 for k in range(4)]
-    z_id = [{"tp": z, "sp": sp} for z in zs]
+    side = tp // 2
+    inside = tp * (1 - 2 * side) + 3 * side
+    is_end, is_in = inside == 0, inside == 1
+
+    def place(m):
+        return m + side * (3 - 2 * m)
+
+    near, second, far = place(1 - inside), place(2), place(3)
+
+    def zdev(z):
+        return {"tp": z, "sp": sp}
+
     dim = x_buf.shape[1]
     ring = wg_buf.shape[0]
     half = wd_buf.shape[1]
@@ -277,29 +288,77 @@
     for j in range(ndn):
         dn_copy(j).start()
 
+    @pl.when(is_end)
+    def _():
+        z1_buf[2] = jnp.zeros_like(z1_buf[2])
+        z2_buf[2] = jnp.zeros_like(z2_buf[2])
+
     bar = pltpu.get_barrier_semaphore()
-    for dev in [mate] + plane_id[1:] + z_id[1:]:
+    for dev in [mate] + plane_id[1:] + [zdev((tp + k) % 4) for k in (1, 2, 3)]:
         pl.semaphore_signal(bar, inc=1, device_id=dev, device_id_type=MESH)
     pl.semaphore_wait(bar, 7)
 
-    def send(src, dst, ssem, rsem, dev):
-        cp = pltpu.make_async_remote_copy(src_ref=src, dst_ref=dst, send_sem=ssem, recv_sem=rsem, device_id=dev, device_id_type=MESH)
-        cp.start()
-        return cp
+    drains = []
+
+    def send(src, dst, ssem, rsem, dev, cond=None):
+        def make():
+            return pltpu.make_async_remote_copy(src_ref=src, dst_ref=dst, send_sem=ssem, recv_sem=rsem, device_id=dev, device_id_type=MESH)
+
+        def go():
+            make().start()
+
+        def done():
+            make().wait_send()
+
+        if cond is None:
+            go()
+            drains.append(done)
+        else:
+            pl.when(cond)(go)
+            drains.append(lambda: pl.when(cond)(done))
+
+    def landed(ref, rsem):
+        pltpu.make_async_copy(ref, ref, rsem).wait()
 
     order = [1, 2, 3, 0]
-    d1 = {k: send(att_ref.at[pl.ds(4 * plane[k] + 2 * (1 - core), 2)], d1_buf.at[k], d1s.at[k], d1r.at[k], mate) for k in order}
-    r1 = {}
     for k in order:
-        d1[k].wait_recv()
+        send(att_ref.at[pl.ds(4 * plane[k] + 2 * (1 - core), 2)], d1_buf.at[k], d1s.at[k], d1r.at[k], mate)
+    for k in order:
+        landed(d1_buf.at[k], d1r.at[k])
         for h in range(2):
             merge([att_ref.at[4 * plane[k] + 2 * core + h], d1_buf.at[k, h]], m_buf.at[k, h], False)
         if k:
-            r1[k] = send(m_buf.at[k], r1_buf.at[k - 1], r1s.at[k - 1], r1r.at[k - 1], plane_id[k])
+            send(m_buf.at[k], r1_buf.at[k - 1], r1s.at[k - 1], r1r.at[k - 1], plane_id[k])
     for k in (1, 2, 3):
-        r1[k].wait_recv()
+        landed(r1_buf.at[k - 1], r1r.at[k - 1])
     for h in range(2):
         merge([m_buf.at[0, h]] + [r1_buf.at[k, h] for k in range(3)], o_buf.at[pl.ds(128 * h, 128)], True)
+
+    def rows8(z):
+        return pl.ds(pl.multiple_of(8 * z, 8), 8)
+
+    def scatter(j, cols, src, buf, agg, ss, rs):
+        send(src.at[rows8(second), cols], buf.at[2 - inside, :, cols], ss.at[j, 0], rs.at[j, 2 - inside], zdev(second))
+        send(src.at[rows8(far), cols], agg.at[:, cols], ss.at[j, 1], rs.at[j, 3], zdev(near), is_end)
+        send(src.at[rows8(near), cols], buf.at[0, :, cols], ss.at[j, 2], rs.at[j, 0], zdev(near))
+
+    def relay(j, cols, src, buf, agg, ss, rs):
+        @pl.when(is_in)
+        def _():
+            landed(agg.at[:, cols], rs.at[j, 3])
+            src[rows8(far), cols] = src[rows8(far), cols] + agg[:, cols]
+
+        send(src.at[rows8(far), cols], buf.at[1, :, cols], ss.at[j, 1], rs.at[j, 1], zdev(far), is_in)
+
+    def gathered(j, cols, src, buf, rs):
+        landed(buf.at[0, :, cols], rs.at[j, 0])
+        landed(buf.at[1, :, cols], rs.at[j, 1])
+
+        @pl.when(is_in)
+        def _():
+            landed(buf.at[2, :, cols], rs.at[j, 2])
+
+        return src[rows8(tp), cols] + buf[0, :, cols] + buf[1, :, cols] + buf[2, :, cols]
 
     o = jnp.concatenate([o_buf[pl.ds(h, 32, stride=8), :].astype(BF16) for h in range(8)], axis=1)
     wo_copy.wait()
@@ -309,30 +368,37 @@
         p_buf[:, at] = jnp.dot(o, wo_buf[:, at], preferred_element_type=F32)
         return carry
 
-    lax.fori_loop(0, dim // 512, proj, 0)
-
-    def z_scatter(src, buf, ss, rs):
-        return [send(src.at[pl.ds(pl.multiple_of(8 * zs[k], 8), 8), :], buf.at[k - 1], ss.at[k - 1], rs.at[k - 1], z_id[k]) for k in (1, 2, 3)]
-
-    own = pl.ds(pl.multiple_of(8 * tp, 8), 8)
-    z1 = z_scatter(p_buf, z1_buf, z1s, z1r)
+    parts1 = [pl.ds(i * (dim // 2), dim // 2) for i in range(2)]
+    for i in range(2):
+        lax.fori_loop(i * (dim // 1024), (i + 1) * (dim // 1024), proj, 0)
+        scatter(i, parts1[i], p_buf, z1_buf, a1_buf, z1s, z1r)
+    for i in range(2):
+        relay(i, parts1[i], p_buf, z1_buf, a1_buf, z1s, z1r)
     x_copy.wait()
-    for cp in z1:
-        cp.wait_recv()
-    hid = (x_buf[...].astype(F32) + (p_buf[own, :] + z1_buf[0] + z1_buf[1] + z1_buf[2])).astype(BF16).astype(F32)
-    hid_buf[...] = hid
+    for i in range(2):
+        hid_buf[:, parts1[i]] = (x_buf[:, parts1[i]].astype(F32) + gathered(i, parts1[i], p_buf, z1_buf, z1r)).astype(BF16).astype(F32)
+    hid = hid_buf[...]
     inv = lax.rsqrt(jnp.sum(hid * hid, axis=-1, keepdims=True) * (1.0 / dim) + NORM_EPS)
     mine = core * 4
     h_buf[mine + tp] = (hid * inv * g_ref[...].astype(F32).reshape(1, dim)).astype(BF16).astype(F32)
 
-    hz = [send(h_buf.at[mine + tp], h_buf.at[mine + tp], hs.at[k - 1], hr.at[k - 1], z_id[k]) for k in (1, 2, 3)]
-    hd = [send(h_buf.at[mine + tp], h_buf.at[mine + tp], hds.at[0], hdr.at[0], mate)]
-    for k in (1, 2, 3):
-        hz[k - 1].wait_recv()
-        slot = mine + (tp + 4 - k) % 4
-        hd.append(send(h_buf.at[slot], h_buf.at[slot], hds.at[k], hdr.at[k], mate))
-    for cp in hd:
-        cp.wait_recv()
+    def spread(block, ss, rs, first):
+        send(block(tp), block(tp), ss(first), rs(tp), zdev(second))
+        send(block(tp), block(tp), ss(first + 1), rs(tp), zdev(far), is_in)
+        send(block(tp), block(tp), ss(first + 2), rs(tp), zdev(near))
+
+    def h_block(z):
+        return h_buf.at[mine + z]
+
+    spread(h_block, lambda i: hs.at[i], lambda z: hr.at[z], 0)
+    send(h_block(tp), h_block(tp), hds.at[0], hdr.at[tp], mate)
+    for i, z in enumerate((near, second, far)):
+        landed(h_block(z), hr.at[z])
+        if i == 2:
+            send(h_block(z), h_block(z), hs.at[3], hr.at[z], zdev(near), is_in)
+        send(h_block(z), h_block(z), hds.at[1 + i], hdr.at[z], mate)
+    for z in range(4):
+        landed(h_buf.at[4 * (1 - core) + z], hdr.at[z])
     for i in range(4):
         hb_buf[16 * i : 16 * i + 16, :] = jnp.concatenate([h_buf[2 * i], h_buf[2 * i + 1]], axis=0).astype(BF16)
 
@@ -353,75 +419,101 @@
 
     lax.fori_loop(0, nff, ff, 0)
 
-    def down(j, carry):
-        dn_copy(j).wait()
-        p2_buf[:, pl.ds(pl.multiple_of(j * dcol, dcol), dcol)] = jnp.dot(a_buf[...], wd_buf[j], preferred_element_type=F32)
-        return carry
-
-    lax.fori_loop(0, ndn, down, 0)
-
-    d2 = send(p2_buf.at[pl.ds(pl.multiple_of(32 * (1 - core), 32), 32), :], d2_buf, d2s, d2r, mate)
-    d2.wait_recv()
-    s2_buf[...] = p2_buf[pl.ds(pl.multiple_of(32 * core, 32), 32), :] + d2_buf[...]
-    z2 = z_scatter(s2_buf, z2_buf, z2s, z2r)
-    for cp in z2:
-        cp.wait_recv()
-
+    nc = CHUNKS
+    width = dim // nc
+    cols = [pl.ds(j * width, width) for j in range(nc)]
     xn = 2 * cy + (1 - cx)
     yn = 2 * (1 - cy) + cx
     dg = 2 * (1 - cy) + (1 - cx)
     xn_id, yn_id = {"tp": tp, "sp": 2 * xn + core}, {"tp": tp, "sp": 2 * yn + core}
-
-    def block(c, k):
-        return yg_buf.at[4 * (2 * c + core) + (tp + k) % 4]
-
-    started = []
-
-    def pass_on(c, k, dev, rs):
-        started.append(send(block(c, k), block(c, k), ys.at[len(started)], rs, dev))
-
-    def landed(c, k, rs):
-        pltpu.make_async_copy(block(c, k), block(c, k), rs).wait()
-
-    yg_buf[4 * sp + tp] = (hid_buf[...] + (s2_buf[own, :] + z2_buf[0] + z2_buf[1] + z2_buf[2])).astype(BF16).astype(F32)
-    for k in (1, 2, 3):
-        pass_on(chip, 0, z_id[k], yr.at[(4 - k) % 4])
-    pass_on(chip, 0, xn_id, yr.at[4])
-    pass_on(chip, 0, yn_id, yr.at[8])
-    pass_on(chip, 0, mate, ydr.at[0])
-
-    def around(k):
-        landed(xn, k, yr.at[4 + k])
-        if k % 2 == 0:
-            pass_on(xn, k, yn_id, yr.at[12 + k])
-        pass_on(xn, k, mate, ydr.at[4 + k])
-        landed(yn, k, yr.at[8 + k])
-        if k % 2 == 1:
-            pass_on(yn, k, xn_id, yr.at[12 + k])
-        pass_on(yn, k, mate, ydr.at[8 + k])
-
-    for k in (1, 2, 3):
-        landed(chip, k, yr.at[k])
-        pass_on(chip, k, xn_id, yr.at[4 + k])
-        pass_on(chip, k, yn_id, yr.at[8 + k])
-        pass_on(chip, k, mate, ydr.at[k])
-        around(k - 1)
-    around(3)
-    for k in range(4):
-        landed(dg, k, yr.at[12 + k])
-        pass_on(dg, k, mate, ydr.at[12 + k])
-    for i, c in enumerate((chip, xn, yn, dg)):
-        for k in range(4):
-            other = yg_buf.at[4 * (2 * c + (1 - core)) + (tp + k) % 4]
-            pltpu.make_async_copy(other, other, ydr.at[4 * i + k]).wait()
-
-    def out(i, carry):
-        y_ref[pl.ds(pl.multiple_of(i * 16, 16), 16), :] = jnp.concatenate([yg_buf[2 * i], yg_buf[2 * i + 1]], axis=0).astype(BF16)
-        return carry
-
-    lax.fori_loop(0, yg_buf.shape[0] // 2, out, 0)
-    for cp in list(d1.values()) + list(r1.values()) + z1 + hz + hd + [d2] + z2 + started:
-        cp.wait_send()
+    zorder = (tp, near, second, far)
+    count = [0] * nc
+
+    def block(j, c, z):
+        return yg_buf.at[4 * (2 * c + core) + z, :, cols[j]]
+
+    def pass_on(j, c, z, dev, rs, cond=None):
+        send(block(j, c, z), block(j, c, z), ys.at[j, count[j]], rs, dev, cond)
+        count[j] += 1
+
+    def down(j):
+        def one(i, carry):
+            dn_copy(i).wait()
+            p2_buf[:, pl.ds(pl.multiple_of(i * dcol, dcol), dcol)] = jnp.dot(a_buf[...], wd_buf[i], preferred_element_type=F32)
+            return carry
+
+        lax.fori_loop(j * ndn // nc, (j + 1) * ndn // nc, one, 0)
+        send(p2_buf.at[pl.ds(pl.multiple_of(32 * (1 - core), 32), 32), cols[j]], d2_buf.at[:, cols[j]], d2s.at[j], d2r.at[j], mate)
+
+    def pair(j):
+        landed(d2_buf.at[:, cols[j]], d2r.at[j])
+        s2_buf[:, cols[j]] = p2_buf[pl.ds(pl.multiple_of(32 * core, 32), 32), cols[j]] + d2_buf[:, cols[j]]
+        scatter(j, cols[j], s2_buf, z2_buf, a2_buf, z2s, z2r)
+
+    def mid(j):
+        relay(j, cols[j], s2_buf, z2_buf, a2_buf, z2s, z2r)
+
+    def own(j):
+        yg_buf[4 * sp + tp, :, cols[j]] = (hid_buf[:, cols[j]] + gathered(j, cols[j], s2_buf, z2_buf, z2r)).astype(BF16).astype(F32)
+        pass_on(j, chip, tp, xn_id, yr.at[j, 4 + tp])
+        pass_on(j, chip, tp, yn_id, yr.at[j, 8 + tp])
+        at = count[j]
+        spread(lambda z: block(j, chip, z), lambda i: ys.at[j, i], lambda z: yr.at[j, z], at)
+        count[j] = at + 3
+        pass_on(j, chip, tp, mate, ydr.at[j, tp])
+
+    def column(j):
+        for i, z in enumerate(zorder[1:]):
+            landed(block(j, chip, z), yr.at[j, z])
+            if i == 2:
+                pass_on(j, chip, z, zdev(near), yr.at[j, z], is_in)
+            pass_on(j, chip, z, xn_id, yr.at[j, 4 + z])
+            pass_on(j, chip, z, yn_id, yr.at[j, 8 + z])
+            pass_on(j, chip, z, mate, ydr.at[j, z])
+
+    def around(j):
+        for i, z in enumerate(zorder):
+            landed(block(j, xn, z), yr.at[j, 4 + z])
+            if i % 2 == 0:
+                pass_on(j, xn, z, yn_id, yr.at[j, 12 + z])
+            pass_on(j, xn, z, mate, ydr.at[j, 4 + z])
+            landed(block(j, yn, z), yr.at[j, 8 + z])
+            if i % 2 == 1:
+                pass_on(j, yn, z, xn_id, yr.at[j, 12 + z])
+            pass_on(j, yn, z, mate, ydr.at[j, 8 + z])
+
+    def across(j):
+        for z in zorder:
+            landed(block(j, dg, z), yr.at[j, 12 + z])
+            pass_on(j, dg, z, mate, ydr.at[j, 12 + z])
+
+    def out_copy(j):
+        return pltpu.make_async_copy(yo_buf.at[:, cols[j]], y_hbm.at[:, cols[j]], osem.at[j])
+
+    def finish(j):
+        for i, c in enumerate((chip, xn, yn, dg)):
+            for z in zorder:
+                landed(yg_buf.at[4 * (2 * c + (1 - core)) + z, :, cols[j]], ydr.at[j, 4 * i + z])
+
+        def out(i, carry):
+            yo_buf[pl.ds(pl.multiple_of(i * 16, 16), 16), cols[j]] = jnp.concatenate([yg_buf[2 * i, :, cols[j]], yg_buf[2 * i + 1, :, cols[j]]], axis=0).astype(BF16)
+            return carry
+
+        lax.fori_loop(0, yg_buf.shape[0] // 2, out, 0)
+        out_copy(j).start()
+
+    def run(stages, steps):
+        for t in range(steps):
+            for lag, stage in stages:
+                if 0 <= t - lag < nc:
+                    stage(t - lag)
+
+    run([(0, down), (1, pair), (2, mid)], nc + 2)
+    run([(0, own), (1, column), (2, around), (3, across), (4, finish)], nc + 4)
+    for done in drains:
+        done()
+    for j in range(nc):
+        out_copy(j).wait()
 
 
 def tail(att, x, g, wo, wg, wu, wd):
@@ -434,7 +526,7 @@
         tail_kernel,
         out_shape=jax.ShapeDtypeStruct((batch, dim), BF16),
         in_specs=[VMEM, ANY, VMEM, ANY, ANY, ANY, ANY],
-        out_specs=VMEM,
+        out_specs=ANY,
         scratch_shapes=[
             pltpu.VMEM((4, 2, PART, 128), F32),
             pltpu.VMEM((4, 2, PART, 128), F32),
@@ -442,6 +534,7 @@
             pltpu.VMEM((256, 128), F32),
             pltpu.VMEM((32, dim), F32),
             pltpu.VMEM((3, 8, dim), F32),
+            pltpu.VMEM((8, dim), F32),
             pltpu.VMEM((8, 8, dim), F32),
             pltpu.VMEM((64, dim), BF16),
             pltpu.VMEM((64, half), BF16),
@@ -449,17 +542,19 @@
             pltpu.VMEM((32, dim), F32),
             pltpu.VMEM((32, dim), F32),
             pltpu.VMEM((3, 8, dim), F32),
+            pltpu.VMEM((8, dim), F32),
             pltpu.VMEM((batch // 8, 8, dim), F32),
+            pltpu.VMEM((batch, dim), BF16),
             pltpu.VMEM((8, dim), BF16),
             pltpu.VMEM((8, dim), F32),
             pltpu.VMEM(wo.shape, BF16),
             pltpu.VMEM((ring, dim, BLK), BF16),
             pltpu.VMEM((ring, dim, BLK), BF16),
             pltpu.VMEM((ndn, half, dim // ndn), BF16),
-            dma((2,)), dma((ring,)), dma((ring,)), dma((ndn,)),
-            dma((4,)), dma((4,)), dma((3,)), dma((3,)), dma((3,)), dma((3,)),
-            dma((3,)), dma((3,)), dma((4,)), dma((4,)), dma, dma, dma((3,)), dma((3,)),
-            dma((40,)), dma((16,)), dma((16,)),
+            dma((2,)), dma((ring,)), dma((ring,)), dma((ndn,)), dma((CHUNKS,)),
+            dma((4,)), dma((4,)), dma((3,)), dma((3,)), dma((2, 3)), dma((2, 4)),
+            dma((4,)), dma((4,)), dma((4,)), dma((4,)), dma((CHUNKS,)), dma((CHUNKS,)), dma((CHUNKS, 3)), dma((CHUNKS, 4)),
+            dma((CHUNKS, 34)), dma((CHUNKS, 16)), dma((CHUNKS, 16)),
         ],
         compiler_params=pltpu.CompilerParams(collective_id=0, has_side_effects=True, vmem_limit_bytes=63_000_000),
         cost_estimate=pl.CostEstimate(flops=2 * 64 * dim * half * 3, bytes_accessed=6 * dim * half, transcendentals=0),

time: 127 us -> 119 us (0.937)
  the two profiles are of different devices: /device:TPU:19 before, /device:TPU:1 now
where the time goes in v4:
time: 119 us
  Pallas kernels  115 us (97%)
  local copies, waits for them, and re-layouts  3.13 us (3%)
    pallas_call x1, Pallas kernels, tail(): pl.pallas_call(tail_kernel, out_shape=jax.ShapeDtypeStruct((batch, dim),...  90.7 us
    pallas_call x1, Pallas kernels, front(): pl.pallas_call(front_kernel, out_shape=(jax.ShapeDtypeStruct(k.shape, BF1...  24.1 us
    unnamed x1, local copies, waits for them, and re-layouts  3.13 us

profile of v4, /device:TPU:1, one launch (start us, length us, event | category | flops | bytes accessed | tf_op | source)
XLA Modules:
  0.0 118.6 jit_solution(14494335311637860196)
XLA Ops:
  0.6 24.1 %front.1 = (bf16[256,8,16,128]{3,2,1,0:T(8,128)(2,1)}, bf16[256,8,16,128]{3,2,1,0:T(8,128)(2,1)}, f32[16,144,128]{2,1,0:T(8,128)}) custom-call(s32[256]{0:T(256)} %lens_ref.1, bf16[256,4096]{1,0:T(8,128)(2,1)} %x_hbm.3, bf16[4096]{0:T(1024)(128)(2,1)} %g_hbm.1, f32[512,256]{1,0:T(8,128)} %constant.2.clone.tab_hbm, bf16[4096,1024]{1,0:T(8,128)(2,1)} %wq_hbm.1, ...), custom_call_target="tpu_custom_call" | custom-call | flops 3221225472 | bytes 46137344 | tf_op jit(solution)/shard_map/front/pallas_call | solution.py:186
  24.7 90.7 %tail.1 = bf16[256,4096]{1,0:T(8,128)(2,1)} custom-call(f32[16,144,128]{2,1,0:T(8,128)} %get-tuple-element.6.att_ref, bf16[256,4096]{1,0:T(8,128)(2,1)} %x_hbm.3, bf16[4096]{0:T(1024)(128)(2,1)} %g_ref.1, bf16[1024,4096]{1,0:T(8,128)(2,1)} %wo_hbm.1, bf16[4096,3584]{1,0:T(8,128)(2,1)} %wg_hbm.1, bf16[4096,3584]{1,0:T(8,128)(2,1)} %wu_hbm.1, ...), custom_call_target="tpu_custom_call" | custom-call | flops 2818572288 | bytes 44040192 | tf_op jit(solution)/shard_map/tail/pallas_call | solution.py:525
  115.5 3.1 %copy.18 = bf16[256,4096]{1,0:T(8,128)(2,1)} copy(bf16[256,4096]{1,0:T(8,128)(2,1)} %tail.1) | data formatting | bytes 4194304

commit v5 on v4

--- a/solution.py
+++ b/solution.py
@@ -234,8 +234,8 @@
 
 
 def tail_kernel(
-    att_ref, x_hbm, g_ref, wo_hbm, wg_hbm, wu_hbm, wd_hbm, y_hbm,
-    d1_buf, m_buf, r1_buf, o_buf, p_buf, z1_buf, a1_buf, h_buf, hb_buf, a_buf, p2_buf, d2_buf, s2_buf, z2_buf, a2_buf, yg_buf, yo_buf, x_buf, hid_buf,
+    att_hbm, x_hbm, g_hbm, wo_hbm, wg_hbm, wu_hbm, wd_hbm, y_hbm,
+    att_ref, g_ref, d1_buf, m_buf, r1_buf, o_buf, p_buf, z1_buf, a1_buf, h_buf, hb_buf, a_buf, p2_buf, d2_buf, s2_buf, z2_buf, a2_buf, yg_buf, yo_buf, x_buf, hid_buf,
     wo_buf, wg_buf, wu_buf, wd_buf,
     lsem, gsem, usem, dsem, osem, d1s, d1r, r1s, r1r, z1s, z1r, hs, hr, hds, hdr, d2s, d2r, z2s, z2r, ys, yr, ydr,
 ):
@@ -280,13 +280,17 @@
             wd_hbm.at[pl.ds(pl.multiple_of(core * half, BLK), half), pl.ds(pl.multiple_of(j * dcol, dcol), dcol)], wd_buf.at[j], dsem.at[j]
         )
 
+    att_copy = pltpu.make_async_copy(att_hbm, att_ref, lsem.at[2])
+    g_copy = pltpu.make_async_copy(g_hbm, g_ref, lsem.at[3])
+    att_copy.start()
+    x_copy.start()
+    g_copy.start()
     wo_copy.start()
-    x_copy.start()
-    for j in range(min(ring, nff)):
-        for cp in ff_copies(j, j):
-            cp.start()
-    for j in range(ndn):
-        dn_copy(j).start()
+
+    def prefetch_ff(lo, hi):
+        for j in range(lo, min(hi, ring, nff)):
+            for cp in ff_copies(j, j):
+                cp.start()
 
     @pl.when(is_end)
     def _():
@@ -321,6 +325,7 @@
         pltpu.make_async_copy(ref, ref, rsem).wait()
 
     order = [1, 2, 3, 0]
+    att_copy.wait()
     for k in order:
         send(att_ref.at[pl.ds(4 * plane[k] + 2 * (1 - core), 2)], d1_buf.at[k], d1s.at[k], d1r.at[k], mate)
     for k in order:
@@ -329,6 +334,7 @@
             merge([att_ref.at[4 * plane[k] + 2 * core + h], d1_buf.at[k, h]], m_buf.at[k, h], False)
         if k:
             send(m_buf.at[k], r1_buf.at[k - 1], r1s.at[k - 1], r1r.at[k - 1], plane_id[k])
+    prefetch_ff(0, 2)
     for k in (1, 2, 3):
         landed(r1_buf.at[k - 1], r1r.at[k - 1])
     for h in range(2):
@@ -372,9 +378,13 @@
     for i in range(2):
         lax.fori_loop(i * (dim // 1024), (i + 1) * (dim // 1024), proj, 0)
         scatter(i, parts1[i], p_buf, z1_buf, a1_buf, z1s, z1r)
+    prefetch_ff(2, ring)
     for i in range(2):
         relay(i, parts1[i], p_buf, z1_buf, a1_buf, z1s, z1r)
+    for j in range(ndn // 2):
+        dn_copy(j).start()
     x_copy.wait()
+    g_copy.wait()
     for i in range(2):
         hid_buf[:, parts1[i]] = (x_buf[:, parts1[i]].astype(F32) + gathered(i, parts1[i], p_buf, z1_buf, z1r)).astype(BF16).astype(F32)
     hid = hid_buf[...]
@@ -392,6 +402,8 @@
 
     spread(h_block, lambda i: hs.at[i], lambda z: hr.at[z], 0)
     send(h_block(tp), h_block(tp), hds.at[0], hdr.at[tp], mate)
+    for j in range(ndn // 2, ndn):
+        dn_copy(j).start()
     for i, z in enumerate((near, second, far)):
         landed(h_block(z), hr.at[z])
         if i == 2:
@@ -519,15 +531,17 @@
 def tail(att, x, g, wo, wg, wu, wd):
     batch, dim = x.shape
     half = wg.shape[1] // 2
-    ring = min(4, half // BLK)
+    ring = min(5, half // BLK)
     ndn = 8
     dma = pltpu.SemaphoreType.DMA
     return pl.pallas_call(
         tail_kernel,
         out_shape=jax.ShapeDtypeStruct((batch, dim), BF16),
-        in_specs=[VMEM, ANY, VMEM, ANY, ANY, ANY, ANY],
+        in_specs=[ANY] * 7,
         out_specs=ANY,
         scratch_shapes=[
+            pltpu.VMEM(att.shape, F32),
+            pltpu.VMEM((dim,), BF16),
             pltpu.VMEM((4, 2, PART, 128), F32),
             pltpu.VMEM((4, 2, PART, 128), F32),
             pltpu.VMEM((3, 2, PART, 128), F32),
@@ -551,7 +565,7 @@
             pltpu.VMEM((ring, dim, BLK), BF16),
             pltpu.VMEM((ring, dim, BLK), BF16),
             pltpu.VMEM((ndn, half, dim // ndn), BF16),
-            dma((2,)), dma((ring,)), dma((ring,)), dma((ndn,)), dma((CHUNKS,)),
+            dma((4,)), dma((ring,)), dma((ring,)), dma((ndn,)), dma((CHUNKS,)),
             dma((4,)), dma((4,)), dma((3,)), dma((3,)), dma((2, 3)), dma((2, 4)),
             dma((4,)), dma((4,)), dma((4,)), dma((4,)), dma((CHUNKS,)), dma((CHUNKS,)), dma((CHUNKS, 3)), dma((CHUNKS, 4)),
             dma((CHUNKS, 34)), dma((CHUNKS, 16)), dma((CHUNKS, 16)),
@@ -562,6 +576,33 @@
     )(att, x, g, wo, wg, wu, wd)
 
 
+def land_kernel(y_hbm, out_hbm, buf, isem, osem):
+    n = isem.shape[0]
+    rows = buf.shape[0] // n
+    ats = [pl.ds(i * rows, rows) for i in range(n)]
+    ins = [pltpu.make_async_copy(y_hbm.at[at, :], buf.at[at, :], isem.at[i]) for i, at in enumerate(ats)]
+    outs = [pltpu.make_async_copy(buf.at[at, :], out_hbm.at[at, :], osem.at[i]) for i, at in enumerate(ats)]
+    for cp in ins:
+        cp.start()
+    for a, b in zip(ins, outs):
+        a.wait()
+        b.start()
+    for cp in outs:
+        cp.wait()
+
+
+def land(y):
+    return pl.pallas_call(
+        land_kernel,
+        out_shape=jax.ShapeDtypeStruct(y.shape, y.dtype),
+        in_specs=[ANY],
+        out_specs=ANY,
+        scratch_shapes=[pltpu.VMEM(y.shape, y.dtype), pltpu.SemaphoreType.DMA((4,)), pltpu.SemaphoreType.DMA((4,))],
+        compiler_params=pltpu.CompilerParams(vmem_limit_bytes=63_000_000),
+        name="land",
+    )(y)
+
+
 def rope_table(length):
     freq = np.power(ROPE_BASE, np.arange(64) * (-2.0 / 128)).astype(np.float32)
     angles = (np.arange(length, dtype=np.float32)[:, None] * freq).astype(np.float64)
@@ -580,6 +621,6 @@
         shape = (batch, 8, 16, 128)
         k_out, v_out, att = front(seq_lens, x_tok, g_attn, rope_table(k_blk.shape[1] * mesh.shape["sp"]), wq, wk, wv, k_blk.reshape(shape), v_blk.reshape(shape))
         y = tail(att, x_tok, g_mlp, wo, wg, wu, wd)
-        return y, k_out.reshape(k_blk.shape), v_out.reshape(v_blk.shape)
+        return land(y), k_out.reshape(k_blk.shape), v_out.reshape(v_blk.shape)
 
     return jax.shard_map(local_step, mesh=mesh, in_specs=(full_spec, full_spec, cache_spec, cache_spec, full_spec, col_spec, col_spec, col_spec, row_spec, full_spec, col_spec, col_spec, row_spec), out_specs=(full_spec, cache_spec, cache_spec), check_vma=False)

time: 119 us -> 117 us (0.983)
  local copies, waits for them, and re-layouts: 3.13 us -> 0 us
    unnamed x1 -> x0, local copies, waits for them, and re-layouts: 3.13 us -> none
    pallas_call x0 -> x1, Pallas kernels: none -> 2.42 us  [land(): pl.pallas_call(land_kernel, out_shape=jax.ShapeDtypeStruct(y.shape, y.dty...]
    pallas_call x1, Pallas kernels: 90.7 us -> 89.3 us  [tail(): pl.pallas_call(tail_kernel, out_shape=jax.ShapeDtypeStruct((batch, dim),...]
where the time goes in v5:
time: 117 us; the launch traced here: 116 us
  Pallas kernels  116 us (99%)
    pallas_call x1, Pallas kernels, tail(): pl.pallas_call(tail_kernel, out_shape=jax.ShapeDtypeStruct((batch, dim),...  89.3 us
    pallas_call x1, Pallas kernels, front(): pl.pallas_call(front_kernel, out_shape=(jax.ShapeDtypeStruct(k.shape, BF1...  24.1 us
    pallas_call x1, Pallas kernels, land(): pl.pallas_call(land_kernel, out_shape=jax.ShapeDtypeStruct(y.shape, y.dty...  2.42 us

profile of v5, /device:TPU:1, one launch (start us, length us, event | category | flops | bytes accessed | tf_op | source)
XLA Modules:
  0.0 116.4 jit_solution(8423957116552949909)
XLA Ops:
  0.6 24.1 %front.1 = (bf16[256,8,16,128]{3,2,1,0:T(8,128)(2,1)}, bf16[256,8,16,128]{3,2,1,0:T(8,128)(2,1)}, f32[16,144,128]{2,1,0:T(8,128)}) custom-call(s32[256]{0:T(256)} %lens_ref.1, bf16[256,4096]{1,0:T(8,128)(2,1)} %x_hbm.3, bf16[4096]{0:T(1024)(128)(2,1)} %g_hbm.2, f32[512,256]{1,0:T(8,128)} %constant.2.clone.tab_hbm, bf16[4096,1024]{1,0:T(8,128)(2,1)} %wq_hbm.1, ...), custom_call_target="tpu_custom_call" | custom-call | flops 3221225472 | bytes 46137344 | tf_op jit(solution)/shard_map/front/pallas_call | solution.py:186
  24.7 89.3 %tail.1.y_hbm = bf16[256,4096]{1,0:T(8,128)(2,1)} custom-call(f32[16,144,128]{2,1,0:T(8,128)} %get-tuple-element.6.att_hbm, bf16[256,4096]{1,0:T(8,128)(2,1)} %x_hbm.3, bf16[4096]{0:T(1024)(128)(2,1)} %g_hbm.3, bf16[1024,4096]{1,0:T(8,128)(2,1)} %wo_hbm.1, bf16[4096,3584]{1,0:T(8,128)(2,1)} %wg_hbm.1, bf16[4096,3584]{1,0:T(8,128)(2,1)} %wu_hbm.1, ...), custom_call_target="tpu_custom_call" | custom-call | flops 2818572288 | bytes 44040192 | tf_op jit(solution)/shard_map/tail/pallas_call | solution.py:537
  114.0 2.4 %land.1 = bf16[256,4096]{1,0:T(8,128)(2,1)} custom-call(bf16[256,4096]{1,0:T(8,128)(2,1)} %tail.1.y_hbm), custom_call_target="tpu_custom_call" | custom-call | tf_op jit(solution)/shard_map/land/pallas_call | solution.py:595

commit v6 on v5

--- a/solution.py
+++ b/solution.py
@@ -44,9 +44,7 @@
         pltpu.make_async_copy(wk_hbm, w_buf.at[nq, :, pl.ds(0, BLK)], wsem.at[nq]),
         pltpu.make_async_copy(wv_hbm, w_buf.at[nq, :, pl.ds(BLK, BLK)], wsem.at[nq + 1]),
     ])
-    for cps in w_copies:
-        for cp in cps:
-            cp.start()
+    w_copies[0][0].start()
 
     def cache_copies(g):
         at = pl.ds(g * nreq, nreq)
@@ -65,12 +63,17 @@
     def part_copy(g):
         return pltpu.make_async_copy(out_buf.at[pl.ds(2 * g, 2)], out_hbm.at[pl.ds(2 * g, 2)], osem.at[2, g])
 
-    for g in range(groups):
-        for cp in cache_copies(g):
-            cp.start()
+    def fetch(lo, hi):
+        for g in range(lo, hi):
+            for cp in cache_copies(g):
+                cp.start()
+
     g_copy.wait()
     gain = g_buf[...].astype(F32).reshape(1, dim)
     x_copy.wait()
+    for cps in w_copies[1:]:
+        for cp in cps:
+            cp.start()
 
     def norm(i, carry):
         at = pl.ds(pl.multiple_of(i * 16, 16), 16)
@@ -97,6 +100,7 @@
     for i in range(nq + 1):
         for cp in w_copies[i]:
             cp.wait()
+        fetch(groups * i // (nq + 1), groups * (i + 1) // (nq + 1))
         prod = jnp.dot(u_buf[...], w_buf[i], preferred_element_type=F32)
         for s in range(4):
             part = prod[:, s * 128 : (s + 1) * 128]
@@ -237,7 +241,7 @@
     att_hbm, x_hbm, g_hbm, wo_hbm, wg_hbm, wu_hbm, wd_hbm, y_hbm,
     att_ref, g_ref, d1_buf, m_buf, r1_buf, o_buf, p_buf, z1_buf, a1_buf, h_buf, hb_buf, a_buf, p2_buf, d2_buf, s2_buf, z2_buf, a2_buf, yg_buf, yo_buf, x_buf, hid_buf,
     wo_buf, wg_buf, wu_buf, wd_buf,
-    lsem, gsem, usem, dsem, osem, d1s, d1r, r1s, r1r, z1s, z1r, hs, hr, hds, hdr, d2s, d2r, z2s, z2r, ys, yr, ydr,
+    lsem, gsem, usem, dsem, osem, d1s, d1r, r1s, r1r, z1s, z1r, hs, hr, hds, hdr, d2s, d2r, z2s, z2r, ys, yr, ydr, turn,
 ):
     tp, sp = lax.axis_index("tp"), lax.axis_index("sp")
     core, chip = sp % 2, sp // 2
@@ -332,8 +336,23 @@
         landed(d1_buf.at[k], d1r.at[k])
         for h in range(2):
             merge([att_ref.at[4 * plane[k] + 2 * core + h], d1_buf.at[k, h]], m_buf.at[k, h], False)
-        if k:
-            send(m_buf.at[k], r1_buf.at[k - 1], r1s.at[k - 1], r1r.at[k - 1], plane_id[k])
+
+    @pl.when(core == 1)
+    def _():
+        pl.semaphore_wait(turn, 1)
+
+    before = len(drains)
+    for k in (1, 2, 3):
+        send(m_buf.at[k], r1_buf.at[k - 1], r1s.at[k - 1], r1r.at[k - 1], plane_id[k])
+    plane_sent = drains[before:]
+    del drains[before:]
+
+    @pl.when(core == 0)
+    def _():
+        for done in plane_sent:
+            done()
+        pl.semaphore_signal(turn, inc=1, device_id=mate, device_id_type=MESH)
+
     prefetch_ff(0, 2)
     for k in (1, 2, 3):
         landed(r1_buf.at[k - 1], r1r.at[k - 1])
@@ -524,6 +543,12 @@
     run([(0, own), (1, column), (2, around), (3, across), (4, finish)], nc + 4)
     for done in drains:
         done()
+
+    @pl.when(core == 1)
+    def _():
+        for done in plane_sent:
+            done()
+
     for j in range(nc):
         out_copy(j).wait()
 
@@ -568,7 +593,7 @@
             dma((4,)), dma((ring,)), dma((ring,)), dma((ndn,)), dma((CHUNKS,)),
             dma((4,)), dma((4,)), dma((3,)), dma((3,)), dma((2, 3)), dma((2, 4)),
             dma((4,)), dma((4,)), dma((4,)), dma((4,)), dma((CHUNKS,)), dma((CHUNKS,)), dma((CHUNKS, 3)), dma((CHUNKS, 4)),
-            dma((CHUNKS, 34)), dma((CHUNKS, 16)), dma((CHUNKS, 16)),
+            dma((CHUNKS, 34)), dma((CHUNKS, 16)), dma((CHUNKS, 16)), pltpu.SemaphoreType.REGULAR,
         ],
         compiler_params=pltpu.CompilerParams(collective_id=0, has_side_effects=True, vmem_limit_bytes=63_000_000),
         cost_estimate=pl.CostEstimate(flops=2 * 64 * dim * half * 3, bytes_accessed=6 * dim * half, transcendentals=0),

time: 117 us -> 106 us (0.906)
  Pallas kernels: 116 us -> 106 us
    pallas_call x1, Pallas kernels: 24.1 us -> 17.4 us  [front(): pl.pallas_call(front_kernel, out_shape=(jax.ShapeDtypeStruct(k.shape, BF1...]
    pallas_call x1, Pallas kernels: 89.3 us -> 85.7 us  [tail(): pl.pallas_call(tail_kernel, out_shape=jax.ShapeDtypeStruct((batch, dim),...]
where the time goes in v6:
time: 106 us
  Pallas kernels  106 us (100%)
    pallas_call x1, Pallas kernels, tail(): pl.pallas_call(tail_kernel, out_shape=jax.ShapeDtypeStruct((batch, dim),...  85.7 us
    pallas_call x1, Pallas kernels, front(): pl.pallas_call(front_kernel, out_shape=(jax.ShapeDtypeStruct(k.shape, BF1...  17.4 us
    pallas_call x1, Pallas kernels, land(): pl.pallas_call(land_kernel, out_shape=jax.ShapeDtypeStruct(y.shape, y.dty...  2.42 us

profile of v6, /device:TPU:1, one launch (start us, length us, event | category | flops | bytes accessed | tf_op | source)
XLA Modules:
  0.0 106.2 jit_solution(16103386320799420005)
XLA Ops:
  0.6 17.4 %front.1 = (bf16[256,8,16,128]{3,2,1,0:T(8,128)(2,1)}, bf16[256,8,16,128]{3,2,1,0:T(8,128)(2,1)}, f32[16,144,128]{2,1,0:T(8,128)}) custom-call(s32[256]{0:T(256)} %lens_ref.1, bf16[256,4096]{1,0:T(8,128)(2,1)} %x_hbm.3, bf16[4096]{0:T(1024)(128)(2,1)} %g_hbm.2, f32[512,256]{1,0:T(8,128)} %constant.2.clone.tab_hbm, bf16[4096,1024]{1,0:T(8,128)(2,1)} %wq_hbm.1, ...), custom_call_target="tpu_custom_call" | custom-call | flops 3221225472 | bytes 46137344 | tf_op jit(solution)/shard_map/front/pallas_call | solution.py:190
  18.1 85.7 %tail.1.y_hbm = bf16[256,4096]{1,0:T(8,128)(2,1)} custom-call(f32[16,144,128]{2,1,0:T(8,128)} %get-tuple-element.6.att_hbm, bf16[256,4096]{1,0:T(8,128)(2,1)} %x_hbm.3, bf16[4096]{0:T(1024)(128)(2,1)} %g_hbm.3, bf16[1024,4096]{1,0:T(8,128)(2,1)} %wo_hbm.1, bf16[4096,3584]{1,0:T(8,128)(2,1)} %wg_hbm.1, bf16[4096,3584]{1,0:T(8,128)(2,1)} %wu_hbm.1, ...), custom_call_target="tpu_custom_call" | custom-call | flops 2818572288 | bytes 44040192 | tf_op jit(solution)/shard_map/tail/pallas_call | solution.py:562
  103.8 2.4 %land.1 = bf16[256,4096]{1,0:T(8,128)(2,1)} custom-call(bf16[256,4096]{1,0:T(8,128)(2,1)} %tail.1.y_hbm), custom_call_target="tpu_custom_call" | custom-call | tf_op jit(solution)/shard_map/land/pallas_call | solution.py:620

commit v7 on v6

--- a/solution.py
+++ b/solution.py
@@ -18,6 +18,7 @@
 NEG = -1e30
 BLK = 256
 CHUNKS = 4
+LEAD = 3
 PART = 144
 
 
@@ -289,7 +290,6 @@
     att_copy.start()
     x_copy.start()
     g_copy.start()
-    wo_copy.start()
 
     def prefetch_ff(lo, hi):
         for j in range(lo, min(hi, ring, nff)):
@@ -330,6 +330,7 @@
 
     order = [1, 2, 3, 0]
     att_copy.wait()
+    wo_copy.start()
     for k in order:
         send(att_ref.at[pl.ds(4 * plane[k] + 2 * (1 - core), 2)], d1_buf.at[k], d1s.at[k], d1r.at[k], mate)
     for k in order:
@@ -533,14 +534,32 @@
         lax.fori_loop(0, yg_buf.shape[0] // 2, out, 0)
         out_copy(j).start()
 
-    def run(stages, steps):
-        for t in range(steps):
-            for lag, stage in stages:
-                if 0 <= t - lag < nc:
-                    stage(t - lag)
-
-    run([(0, down), (1, pair), (2, mid)], nc + 2)
-    run([(0, own), (1, column), (2, around), (3, across), (4, finish)], nc + 4)
+    down(0)
+    for j in range(nc + 4):
+        if j == 0:
+            for i in range(1, nc + 1):
+                if i < nc:
+                    down(i)
+                if i <= LEAD:
+                    pair(i - 1)
+                if 2 <= i <= LEAD + 1:
+                    mid(i - 2)
+        if j < nc:
+            own(j)
+        if j + LEAD < nc:
+            pair(j + LEAD)
+        if 1 <= j and j + LEAD - 1 < nc:
+            if j <= nc:
+                column(j - 1)
+            mid(j + LEAD - 1)
+        elif 1 <= j <= nc:
+            column(j - 1)
+        if 2 <= j <= nc + 1:
+            around(j - 2)
+        if 3 <= j <= nc + 2:
+            across(j - 3)
+        if 4 <= j:
+            finish(j - 4)
     for done in drains:
         done()
 

time: 106 us -> 105 us (level)
  Pallas kernels: 106 us -> 104 us
    pallas_call x1, Pallas kernels: 85.7 us -> 84 us  [tail(): pl.pallas_call(tail_kernel, out_shape=jax.ShapeDtypeStruct((batch, dim),...]
where the time goes in v7:
time: 105 us
  Pallas kernels  104 us (99%)
    pallas_call x1, Pallas kernels, tail(): pl.pallas_call(tail_kernel, out_shape=jax.ShapeDtypeStruct((batch, dim),...  84 us
    pallas_call x1, Pallas kernels, front(): pl.pallas_call(front_kernel, out_shape=(jax.ShapeDtypeStruct(k.shape, BF1...  17.4 us
    pallas_call x1, Pallas kernels, land(): pl.pallas_call(land_kernel, out_shape=jax.ShapeDtypeStruct(y.shape, y.dty...  2.42 us

profile of v7, /device:TPU:1, one launch (start us, length us, event | category | flops | bytes accessed | tf_op | source)
XLA Modules:
  0.0 104.5 jit_solution(6696401070628411342)
XLA Ops:
  0.6 17.4 %front.1 = (bf16[256,8,16,128]{3,2,1,0:T(8,128)(2,1)}, bf16[256,8,16,128]{3,2,1,0:T(8,128)(2,1)}, f32[16,144,128]{2,1,0:T(8,128)}) custom-call(s32[256]{0:T(256)} %lens_ref.1, bf16[256,4096]{1,0:T(8,128)(2,1)} %x_hbm.3, bf16[4096]{0:T(1024)(128)(2,1)} %g_hbm.2, f32[512,256]{1,0:T(8,128)} %constant.2.clone.tab_hbm, bf16[4096,1024]{1,0:T(8,128)(2,1)} %wq_hbm.1, ...), custom_call_target="tpu_custom_call" | custom-call | flops 3221225472 | bytes 46137344 | tf_op jit(solution)/shard_map/front/pallas_call | solution.py:191
  18.1 84.0 %tail.1.y_hbm = bf16[256,4096]{1,0:T(8,128)(2,1)} custom-call(f32[16,144,128]{2,1,0:T(8,128)} %get-tuple-element.6.att_hbm, bf16[256,4096]{1,0:T(8,128)(2,1)} %x_hbm.3, bf16[4096]{0:T(1024)(128)(2,1)} %g_hbm.3, bf16[1024,4096]{1,0:T(8,128)(2,1)} %wo_hbm.1, bf16[4096,3584]{1,0:T(8,128)(2,1)} %wg_hbm.1, bf16[4096,3584]{1,0:T(8,128)(2,1)} %wu_hbm.1, ...), custom_call_target="tpu_custom_call" | custom-call | flops 2818572288 | bytes 44040192 | tf_op jit(solution)/shard_map/tail/pallas_call | solution.py:581
  102.1 2.4 %land.1 = bf16[256,4096]{1,0:T(8,128)(2,1)} custom-call(bf16[256,4096]{1,0:T(8,128)(2,1)} %tail.1.y_hbm), custom_call_target="tpu_custom_call" | custom-call | tf_op jit(solution)/shard_map/land/pallas_call | solution.py:639

commit v8 on v6

--- a/solution.py
+++ b/solution.py
@@ -17,7 +17,9 @@
 VMEM = pl.BlockSpec(memory_space=pltpu.VMEM)
 NEG = -1e30
 BLK = 256
-CHUNKS = 4
+CHUNKS = 8
+LEAD = 5
+LAGS = (2, 4, 5, 6)
 PART = 144
 
 
@@ -289,7 +291,6 @@
     att_copy.start()
     x_copy.start()
     g_copy.start()
-    wo_copy.start()
 
     def prefetch_ff(lo, hi):
         for j in range(lo, min(hi, ring, nff)):
@@ -330,6 +331,7 @@
 
     order = [1, 2, 3, 0]
     att_copy.wait()
+    wo_copy.start()
     for k in order:
         send(att_ref.at[pl.ds(4 * plane[k] + 2 * (1 - core), 2)], d1_buf.at[k], d1s.at[k], d1r.at[k], mate)
     for k in order:
@@ -491,7 +493,13 @@
         at = count[j]
         spread(lambda z: block(j, chip, z), lambda i: ys.at[j, i], lambda z: yr.at[j, z], at)
         count[j] = at + 3
-        pass_on(j, chip, tp, mate, ydr.at[j, tp])
+
+    def four(j, c, which):
+        return yg_buf.at[pl.ds(4 * (2 * c + which), 4), :, cols[j]]
+
+    def hand_over(j, c, i):
+        send(four(j, c, core), four(j, c, core), ys.at[j, count[j]], ydr.at[j, i], mate)
+        count[j] += 1
 
     def column(j):
         for i, z in enumerate(zorder[1:]):
@@ -500,31 +508,30 @@
                 pass_on(j, chip, z, zdev(near), yr.at[j, z], is_in)
             pass_on(j, chip, z, xn_id, yr.at[j, 4 + z])
             pass_on(j, chip, z, yn_id, yr.at[j, 8 + z])
-            pass_on(j, chip, z, mate, ydr.at[j, z])
+        hand_over(j, chip, 0)
 
     def around(j):
         for i, z in enumerate(zorder):
             landed(block(j, xn, z), yr.at[j, 4 + z])
             if i % 2 == 0:
                 pass_on(j, xn, z, yn_id, yr.at[j, 12 + z])
-            pass_on(j, xn, z, mate, ydr.at[j, 4 + z])
             landed(block(j, yn, z), yr.at[j, 8 + z])
             if i % 2 == 1:
                 pass_on(j, yn, z, xn_id, yr.at[j, 12 + z])
-            pass_on(j, yn, z, mate, ydr.at[j, 8 + z])
+        hand_over(j, xn, 1)
+        hand_over(j, yn, 2)
 
     def across(j):
         for z in zorder:
             landed(block(j, dg, z), yr.at[j, 12 + z])
-            pass_on(j, dg, z, mate, ydr.at[j, 12 + z])
+        hand_over(j, dg, 3)
 
     def out_copy(j):
         return pltpu.make_async_copy(yo_buf.at[:, cols[j]], y_hbm.at[:, cols[j]], osem.at[j])
 
     def finish(j):
         for i, c in enumerate((chip, xn, yn, dg)):
-            for z in zorder:
-                landed(yg_buf.at[4 * (2 * c + (1 - core)) + z, :, cols[j]], ydr.at[j, 4 * i + z])
+            landed(four(j, c, 1 - core), ydr.at[j, i])
 
         def out(i, carry):
             yo_buf[pl.ds(pl.multiple_of(i * 16, 16), 16), cols[j]] = jnp.concatenate([yg_buf[2 * i, :, cols[j]], yg_buf[2 * i + 1, :, cols[j]]], axis=0).astype(BF16)
@@ -533,14 +540,20 @@
         lax.fori_loop(0, yg_buf.shape[0] // 2, out, 0)
         out_copy(j).start()
 
-    def run(stages, steps):
-        for t in range(steps):
-            for lag, stage in stages:
-                if 0 <= t - lag < nc:
-                    stage(t - lag)
-
-    run([(0, down), (1, pair), (2, mid)], nc + 2)
-    run([(0, own), (1, column), (2, around), (3, across), (4, finish)], nc + 4)
+    down(0)
+    for i in range(1, max(nc, LEAD + 2)):
+        if i < nc:
+            down(i)
+        if i <= LEAD:
+            pair(i - 1)
+        if 2 <= i <= LEAD + 1:
+            mid(i - 2)
+    stages = [(0, own), (-LEAD, pair), (LAGS[0], column), (1 - LEAD, mid), (LAGS[1], around), (LAGS[2], across), (LAGS[3], finish)]
+    for t in range(nc + LAGS[3]):
+        for lag, stage in stages:
+            j = t - lag
+            if j < nc and (j >= 0 if lag >= 0 else j >= LEAD):
+                stage(j)
     for done in drains:
         done()
 
@@ -593,7 +606,7 @@
             dma((4,)), dma((ring,)), dma((ring,)), dma((ndn,)), dma((CHUNKS,)),
             dma((4,)), dma((4,)), dma((3,)), dma((3,)), dma((2, 3)), dma((2, 4)),
             dma((4,)), dma((4,)), dma((4,)), dma((4,)), dma((CHUNKS,)), dma((CHUNKS,)), dma((CHUNKS, 3)), dma((CHUNKS, 4)),
-            dma((CHUNKS, 34)), dma((CHUNKS, 16)), dma((CHUNKS, 16)), pltpu.SemaphoreType.REGULAR,
+            dma((CHUNKS, 22)), dma((CHUNKS, 16)), dma((CHUNKS, 4)), pltpu.SemaphoreType.REGULAR,
         ],
         compiler_params=pltpu.CompilerParams(collective_id=0, has_side_effects=True, vmem_limit_bytes=63_000_000),
         cost_estimate=pl.CostEstimate(flops=2 * 64 * dim * half * 3, bytes_accessed=6 * dim * half, transcendentals=0),

time: 106 us -> 108 us (1.019)
    pallas_call x1, Pallas kernels: 85.7 us -> 87 us  [tail(): pl.pallas_call(tail_kernel, out_shape=jax.ShapeDtypeStruct((batch, dim),...]
where the time goes in v8:
time: 108 us
  Pallas kernels  107 us (99%)
    pallas_call x1, Pallas kernels, tail(): pl.pallas_call(tail_kernel, out_shape=jax.ShapeDtypeStruct((batch, dim),...  87 us
    pallas_call x1, Pallas kernels, front(): pl.pallas_call(front_kernel, out_shape=(jax.ShapeDtypeStruct(k.shape, BF1...  17.4 us
    pallas_call x1, Pallas kernels, land(): pl.pallas_call(land_kernel, out_shape=jax.ShapeDtypeStruct(y.shape, y.dty...  2.42 us

profile of v8, /device:TPU:1, one launch (start us, length us, event | category | flops | bytes accessed | tf_op | source)
XLA Modules:
  0.0 107.5 jit_solution(15976517321867180415)
XLA Ops:
  0.6 17.4 %front.1 = (bf16[256,8,16,128]{3,2,1,0:T(8,128)(2,1)}, bf16[256,8,16,128]{3,2,1,0:T(8,128)(2,1)}, f32[16,144,128]{2,1,0:T(8,128)}) custom-call(s32[256]{0:T(256)} %lens_ref.1, bf16[256,4096]{1,0:T(8,128)(2,1)} %x_hbm.3, bf16[4096]{0:T(1024)(128)(2,1)} %g_hbm.2, f32[512,256]{1,0:T(8,128)} %constant.2.clone.tab_hbm, bf16[4096,1024]{1,0:T(8,128)(2,1)} %wq_hbm.1, ...), custom_call_target="tpu_custom_call" | custom-call | flops 3221225472 | bytes 46137344 | tf_op jit(solution)/shard_map/front/pallas_call | solution.py:192
  18.1 87.0 %tail.1.y_hbm = bf16[256,4096]{1,0:T(8,128)(2,1)} custom-call(f32[16,144,128]{2,1,0:T(8,128)} %get-tuple-element.6.att_hbm, bf16[256,4096]{1,0:T(8,128)(2,1)} %x_hbm.3, bf16[4096]{0:T(1024)(128)(2,1)} %g_hbm.3, bf16[1024,4096]{1,0:T(8,128)(2,1)} %wo_hbm.1, bf16[4096,3584]{1,0:T(8,128)(2,1)} %wg_hbm.1, bf16[4096,3584]{1,0:T(8,128)(2,1)} %wu_hbm.1, ...), custom_call_target="tpu_custom_call" | custom-call | flops 2818572288 | bytes 44040192 | tf_op jit(solution)/shard_map/tail/pallas_call | solution.py:575
  105.1 2.4 %land.1 = bf16[256,4096]{1,0:T(8,128)(2,1)} custom-call(bf16[256,4096]{1,0:T(8,128)(2,1)} %tail.1.y_hbm), custom_call_target="tpu_custom_call" | custom-call | tf_op jit(solution)/shard_map/land/pallas_call | solution.py:633

commit v9 on v8

--- a/solution.py
+++ b/solution.py
@@ -17,9 +17,9 @@
 VMEM = pl.BlockSpec(memory_space=pltpu.VMEM)
 NEG = -1e30
 BLK = 256
-CHUNKS = 8
-LEAD = 5
-LAGS = (2, 4, 5, 6)
+CHUNKS = 4
+LEAD = 3
+LAGS = (1, 2, 3, 4)
 PART = 144
 
 

time: 108 us -> 104 us (0.963)
  Pallas kernels: 107 us -> 103 us
    pallas_call x1, Pallas kernels: 87 us -> 83.3 us  [tail(): pl.pallas_call(tail_kernel, out_shape=jax.ShapeDtypeStruct((batch, dim),...]
where the time goes in v9:
time: 104 us
  Pallas kernels  103 us (99%)
    pallas_call x1, Pallas kernels, tail(): pl.pallas_call(tail_kernel, out_shape=jax.ShapeDtypeStruct((batch, dim),...  83.3 us
    pallas_call x1, Pallas kernels, front(): pl.pallas_call(front_kernel, out_shape=(jax.ShapeDtypeStruct(k.shape, BF1...  17.4 us
    pallas_call x1, Pallas kernels, land(): pl.pallas_call(land_kernel, out_shape=jax.ShapeDtypeStruct(y.shape, y.dty...  2.42 us

profile of v9, /device:TPU:1, one launch (start us, length us, event | category | flops | bytes accessed | tf_op | source)
XLA Modules:
  0.0 103.8 jit_solution(11337379037826143336)
XLA Ops:
  0.6 17.4 %front.1 = (bf16[256,8,16,128]{3,2,1,0:T(8,128)(2,1)}, bf16[256,8,16,128]{3,2,1,0:T(8,128)(2,1)}, f32[16,144,128]{2,1,0:T(8,128)}) custom-call(s32[256]{0:T(256)} %lens_ref.1, bf16[256,4096]{1,0:T(8,128)(2,1)} %x_hbm.3, bf16[4096]{0:T(1024)(128)(2,1)} %g_hbm.2, f32[512,256]{1,0:T(8,128)} %constant.2.clone.tab_hbm, bf16[4096,1024]{1,0:T(8,128)(2,1)} %wq_hbm.1, ...), custom_call_target="tpu_custom_call" | custom-call | flops 3221225472 | bytes 46137344 | tf_op jit(solution)/shard_map/front/pallas_call | solution.py:192
  18.1 83.3 %tail.1.y_hbm = bf16[256,4096]{1,0:T(8,128)(2,1)} custom-call(f32[16,144,128]{2,1,0:T(8,128)} %get-tuple-element.6.att_hbm, bf16[256,4096]{1,0:T(8,128)(2,1)} %x_hbm.3, bf16[4096]{0:T(1024)(128)(2,1)} %g_hbm.3, bf16[1024,4096]{1,0:T(8,128)(2,1)} %wo_hbm.1, bf16[4096,3584]{1,0:T(8,128)(2,1)} %wg_hbm.1, bf16[4096,3584]{1,0:T(8,128)(2,1)} %wu_hbm.1, ...), custom_call_target="tpu_custom_call" | custom-call | flops 2818572288 | bytes 44040192 | tf_op jit(solution)/shard_map/tail/pallas_call | solution.py:575
  101.4 2.4 %land.1 = bf16[256,4096]{1,0:T(8,128)(2,1)} custom-call(bf16[256,4096]{1,0:T(8,128)(2,1)} %tail.1.y_hbm), custom_call_target="tpu_custom_call" | custom-call | tf_op jit(solution)/shard_map/land/pallas_call | solution.py:633
